TPU v7x, 32 devices: a whole 2x2x4 slice. The times are simulated.
32 devices in a mesh: row: 4 (over y, x), col: 8 (over z, core).
Axes of the slice: x: 2, y: 2, z: 4, core: 2. Of those that a mesh axis runs over, the one named last changes fastest.
Arguments:
- spectra: bfloat16 [16, 2048, 2048], P('row', None, 'col'), may hold values from -6 to 6
- coupling: float32 [16], replicated, may hold values from 0.2 to 1
Outputs:
- returned_spectra: bfloat16 [16, 2048, 2048], P('row', None, 'col')
All inputs are finite; a program needn't handle non-finite values.
Results may differ from a plain program's by a relative error of at most 0.0079.
Values may be sent and summed in bfloat16 or wider, within the bound.
No kernel may reach another device: no remote copies, remote signals or barrier semaphores. Data moves between devices by JAX's collectives and lax.ppermute only.
A program may use at most 128 MiB of HBM per device.

v0:
```python
import math

import jax
import jax.numpy as jnp
from jax import lax
from jax.sharding import PartitionSpec as P

NX = 3072
NY = 3072
M = 1024


def fourier_rows(mode_count, length, factor):
    wavenumber = jnp.arange(1, mode_count + 1, dtype=jnp.int32)
    position = jnp.arange(length, dtype=jnp.int32)
    residue = wavenumber[:, None] * position[None, :] % length
    angles = residue.astype(jnp.float32) * (2.0 * math.pi / length)
    table = jnp.concatenate([jnp.cos(angles), jnp.sin(angles)], 0) * factor
    return table.astype(jnp.bfloat16)


def ellipse(row_index, column_index, mode_count):
    row_waves = row_index % mode_count + 1
    col_waves = column_index % mode_count + 1
    inside = (
        row_waves[:, None] * row_waves[:, None] + col_waves[None, :] * col_waves[None, :]
        <= mode_count * mode_count
    )
    return inside.astype(jnp.float32)


def on_device(spectra, coupling):
    local_count = spectra.shape[0]
    width_here = spectra.shape[2]
    inverse_y = fourier_rows(M, NY, 1.0 / math.sqrt(M)).T
    inverse_x = fourier_rows(M, NX, 1.0 / math.sqrt(M))
    forward_x = fourier_rows(M, NX, 2.0 * math.sqrt(M) / NX).T
    forward_y = fourier_rows(M, NY, 2.0 * math.sqrt(M) / NY)
    half_done = jnp.einsum(
        "yk,fkc->fyc", inverse_y, spectra, preferred_element_type=jnp.float32
    ).astype(jnp.bfloat16)
    gathered = lax.all_to_all(half_done, "col", split_axis=1, concat_axis=2, tiled=True)
    first_field = lax.axis_index("row") * local_count
    strength = lax.dynamic_slice_in_dim(coupling, first_field, gathered.shape[0])
    gridded = jnp.einsum("fyk,kx->fyx", gathered, inverse_x, preferred_element_type=jnp.float32)
    tendency = (gridded + strength[:, None, None] * gridded * gridded).astype(jnp.bfloat16)
    projected = jnp.einsum(
        "fyx,xk->fyk", tendency, forward_x, preferred_element_type=jnp.float32
    ).astype(jnp.bfloat16)
    returned = lax.all_to_all(projected, "col", split_axis=2, concat_axis=1, tiled=True)
    result = jnp.einsum("ky,fyc->fkc", forward_y, returned, preferred_element_type=jnp.float32)
    columns = lax.axis_index("col") * width_here + jnp.arange(width_here, dtype=jnp.int32)
    inside = ellipse(jnp.arange(2 * M, dtype=jnp.int32), columns, M)
    return (result * inside[None, :, :]).astype(jnp.bfloat16)


def solution(mesh):
    placed = (P("row", None, "col"), P())
    return jax.shard_map(
        on_device, mesh=mesh, in_specs=placed, out_specs=P("row", None, "col"), check_vma=False
    )
```

profile of v0, /device:TPU:0, one launch (start us, length us, event | category | flops | bytes accessed | tf_op | source)
XLA Modules:
  0.0 505.0 jit_solution(3590374729908584467)
XLA Ops:
  0.0 52.6 %fusion.8 = (f32[1024,3072]{0,1:T(8,128)}, f32[1024,3072]{0,1:T(8,128)}) fusion(s32[1024]{0:T(1024)S(1)} %iota_add_fusion), kind=kLoop, calls=%fused_computation.14 | loop fusion | flops 28311552 | bytes 25169920 | tf_op jit(solution)/shard_map/cos | solution.py:18
  52.6 20.9 %convert_bitcast_fusion = bf16[4,3072,256]{2,1,0:T(8,128)(2,1)} fusion(bf16[4,2048,256]{2,1,0:T(8,128)(2,1)} %param.2, f32[1024,3072]{0,1:T(8,128)} %get-tuple-element.6, f32[1024,3072]{0,1:T(8,128)} %get-tuple-element.5), kind=kOutput, calls=%fused_computation.23 | convolution fusion | flops 12906921984 | bytes 35651584 | tf_op jit(solution)/shard_map/yk,fkc->fyc/dot_general | solution.py:39
  73.5 0.0 copy-start
  73.5 10.5 %copy.9 = bf16[4,3072,256]{2,0,1:T(4,128)(2,1)} copy(bf16[4,3072,256]{2,1,0:T(8,128)(2,1)} %convert_bitcast_fusion) | data formatting | bytes 12582912 | tf_op jit(solution)/shard_map/convert_element_type | solution.py:41
  84.0 6.4 %all-to-all-start = ((bf16[4,3072,256]{2,0,1:T(4,128)(2,1)}), bf16[4,3072,256]{2,0,1:T(4,128)(2,1)}, u32[]{:S(2)}, u32[]{:S(2)}) async-start(bf16[4,3072,256]{2,0,1:T(4,128)(2,1)} %copy.9), calls=%async_computation | async-start | bytes 12582912 | tf_op jit(solution)/shard_map/all_to_all | solution.py:42
  90.4 0.0 copy-done
  90.4 0.1 dynamic_slice.3
  90.5 138.9 %all-to-all-done = bf16[4,3072,256]{2,0,1:T(4,128)(2,1)} async-done(((bf16[4,3072,256]{2,0,1:T(4,128)(2,1)}), bf16[4,3072,256]{2,0,1:T(4,128)(2,1)}, u32[]{:S(2)}, u32[]{:S(2)}) %all-to-all-start) | async-done | bytes 6291488 | tf_op jit(solution)/shard_map/all_to_all | solution.py:42
  229.4 9.1 %copy.26 = bf16[4,8,384,256]{3,1,2,0:T(8,128)(2,1)} copy(bf16[4,8,384,256]{3,0,2,1:T(4,128)(2,1)} %bitcast.2) | data formatting | bytes 12582912 | tf_op jit(solution)/shard_map/all_to_all | solution.py:42
  238.5 10.4 %all_to_all.29 = bf16[4,384,2048]{2,1,0:T(8,128)(2,1)} reshape(bf16[4,384,8,256]{3,2,1,0:T(8,128)(2,1)} %bitcast.46) | data formatting | bytes 12582912 | tf_op jit(solution)/shard_map/all_to_all | solution.py:42
  248.9 27.8 %fusion.59 = bf16[4,384,3072]{2,1,0:T(8,128)(2,1)} fusion(bf16[4,384,2048]{2,1,0:T(8,128)(2,1)} %all_to_all.29, f32[4]{0:T(128)S(1)} %dynamic_slice.3, f32[1024,3072]{0,1:T(8,128)} %get-tuple-element.6, f32[1024,3072]{0,1:T(8,128)} %get-tuple-element.5), kind=kOutput, calls=%fused_computation.5.clone.clone.clone.clone.2 | convolution fusion | flops 19365101568 | bytes 40894480 | tf_op jit(solution)/shard_map/fyk,kx->fyx/dot_general | solution.py:45
  276.7 27.5 %fusion.16 = bf16[4,384,2048]{2,1,0:T(8,128)(2,1)} fusion(f32[1024,3072]{0,1:T(8,128)} %get-tuple-element.6, f32[1024,3072]{0,1:T(8,128)} %get-tuple-element.5, bf16[4,384,3072]{2,1,0:T(8,128)(2,1)} %fusion.59), kind=kOutput, calls=%fused_computation.24 | convolution fusion | flops 19349372928 | bytes 40894464 | tf_op jit(solution)/shard_map/fyx,xk->fyk/dot_general | solution.py:47
  304.2 10.7 %copy.13 = bf16[4,384,2048]{1,0,2:T(4,128)(2,1)} copy(bf16[4,384,2048]{2,1,0:T(8,128)(2,1)} %fusion.16) | data formatting | bytes 12582912 | tf_op jit(solution)/shard_map/convert_element_type | solution.py:49
  315.0 4.8 all-to-all-start.1
  319.8 0.3 fusion.19
  320.1 138.6 %all-to-all-done.1 = bf16[4,384,2048]{1,0,2:T(4,128)(2,1)} async-done(((bf16[4,384,2048]{1,0,2:T(4,128)(2,1)}), bf16[4,384,2048]{1,0,2:T(4,128)(2,1)}, u32[]{:S(2)}, u32[]{:S(2)}) %all-to-all-start.1) | async-done | bytes 6291488 | tf_op jit(solution)/shard_map/all_to_all | solution.py:50
  458.7 9.2 %copy.25 = bf16[4,384,8,256]{1,2,3,0:T(8,128)(2,1)} copy(bf16[4,384,8,256]{1,0,3,2:T(4,128)(2,1)} %bitcast.6) | data formatting | bytes 12582912 | tf_op jit(solution)/shard_map/all_to_all | solution.py:50
  467.9 10.4 %all_to_all.33 = bf16[4,3072,256]{1,2,0:T(8,128)(2,1)} reshape(bf16[4,8,384,256]{2,1,3,0:T(8,128)(2,1)} %bitcast.47) | data formatting | bytes 12582912 | tf_op jit(solution)/shard_map/all_to_all | solution.py:50
  478.3 20.5 %fusion.15 = bf16[4,2048,256]{1,2,0:T(8,128)(2,1)} fusion(bf16[4,3072,256]{1,2,0:T(8,128)(2,1)} %all_to_all.33, f32[2048,256]{0,1:T(8,128)S(1)} %fusion.19, f32[1024,3072]{0,1:T(8,128)} %get-tuple-element.6, f32[1024,3072]{0,1:T(8,128)} %get-tuple-element.5), kind=kOutput, calls=%fused_computation.20 | convolution fusion | flops 12907970560 | bytes 37748736 | tf_op jit(solution)/shard_map/ky,fyc->fkc/dot_general | solution.py:51
  498.8 6.2 %copy.16 = bf16[4,2048,256]{2,1,0:T(8,128)(2,1)} copy(bf16[4,2048,256]{1,2,0:T(8,128)(2,1)} %fusion.15) | data formatting | bytes 8388608 | tf_op jit(solution)/shard_map/convert_element_type | solution.py:54
  (3 shorter events, 0.0 us)
Async XLA Ops:
  73.5 16.9 %copy-start = (f32[16]{0:T(128)S(1)}, f32[16]{0:T(128)}, u32[]{:S(2)}) copy-start(f32[16]{0:T(128)} %param.3) | copy-start | bytes 196
  84.0 145.4 %all-to-all-start = ((bf16[4,3072,256]{2,0,1:T(4,128)(2,1)}), bf16[4,3072,256]{2,0,1:T(4,128)(2,1)}, u32[]{:S(2)}, u32[]{:S(2)}) async-start(bf16[4,3072,256]{2,0,1:T(4,128)(2,1)} %copy.9), calls=%async_computation | async-start | bytes 12582912 | tf_op jit(solution)/shard_map/all_to_all | solution.py:42
  315.0 143.7 %all-to-all-start.1 = ((bf16[4,384,2048]{1,0,2:T(4,128)(2,1)}), bf16[4,384,2048]{1,0,2:T(4,128)(2,1)}, u32[]{:S(2)}, u32[]{:S(2)}) async-start(bf16[4,384,2048]{1,0,2:T(4,128)(2,1)} %copy.13), calls=%async_computation.1 | async-start | bytes 12582912 | tf_op jit(solution)/shard_map/all_to_all | solution.py:50
where the time goes:
time: 506 us; the launch traced here: 505 us
  waiting for transfers between devices  278 us (55%)
  matrix products  96.8 us (19%)
  local copies, waits for them, and re-layouts  66.6 us (13%)
  other arithmetic  52.9 us (10%)
  starting transfers between devices  11.1 us (2%)
    all_to_all x1, waiting for transfers between devices, on_device(): lax.all_to_all(half_done, 'col', split_axis=1, concat_axis=2, tiled=True)  139 us
    all_to_all x1, waiting for transfers between devices, on_device(): lax.all_to_all(projected, 'col', split_axis=2, concat_axis=1, tiled=True)  139 us
    cos x1, other arithmetic, fourier_rows(): table = jnp.concatenate([jnp.cos(angles), jnp.sin(angles)], 0) * factor  52.6 us
    dot_general x1, matrix products, on_device(): jnp.einsum('fyk,kx->fyx', gathered, inverse_x, preferred_element_type=jnp...  27.8 us
    dot_general x1, matrix products, on_device(): jnp.einsum('fyx,xk->fyk', tendency, forward_x, preferred_element_type=jnp...  27.5 us
    dot_general x1, matrix products, on_device(): jnp.einsum('yk,fkc->fyc', inverse_y, spectra, preferred_element_type=jnp....  20.9 us
    dot_general x1, matrix products, on_device(): jnp.einsum('ky,fyc->fkc', forward_y, returned, preferred_element_type=jnp...  20.5 us
    all_to_all x2, local copies, waits for them, and re-layouts, on_device(): lax.all_to_all(projected, 'col', split_axis=2, concat_axis=1, tiled=True)  19.6 us
  transfers between devices with their start and end apart: 2, of which 2 were waited for; matrix products, arithmetic and copies ran while one was open for 0% of the time, Pallas kernels for 0%

commit v1 on v0

v1 whole, which is shorter than its diff:
```python
import math

import jax
import jax.numpy as jnp
from jax import lax
from jax.experimental import pallas as pl
from jax.experimental.pallas import tpu as pltpu
from jax.sharding import PartitionSpec as P


NX = 3072
NY = 3072
STEP = 16
EDGE = 64
TILE = 256
BLOCKS = 4
VMEM_MIB = {"inverse_y": 16}
VMEM_MOST = 63
LEVELS = 3


def angle_pair(left, right, length):
    residue = (left[:, None] * right[None, :]) % length
    angles = residue.astype(jnp.float32) * (2.0 * math.pi / length)
    return jnp.cos(angles), jnp.sin(angles)


def dot(a, b):
    return jnp.dot(a, b, preferred_element_type=jnp.float32)


def whole(shape):
    return pl.BlockSpec(shape, lambda *_: (0,) * len(shape))


def call(body, outs, grid, ins, in_specs, out_specs, flops, moved, name, scalars=(), scratch=(), **more):
    return pl.pallas_call(
        body,
        out_shape=outs,
        grid_spec=pltpu.PrefetchScalarGridSpec(
            num_scalar_prefetch=len(scalars),
            grid=grid,
            in_specs=in_specs,
            out_specs=out_specs,
            scratch_shapes=scratch,
        ),
        cost_estimate=pl.CostEstimate(flops=flops, bytes_accessed=moved, transcendentals=0),
        compiler_params=pltpu.CompilerParams(vmem_limit_bytes=VMEM_MIB.get(name, VMEM_MOST) * 2**20),
        **more,
    )(*scalars, *ins)


def pick(cosine, base_cos, base_sin):
    return jnp.where(cosine, base_cos, base_sin), jnp.where(cosine, -base_sin, base_cos)


def spread(first, second, fine_cos, fine_sin, scale):
    return ((first * fine_cos + second * fine_sin) * scale).astype(jnp.bfloat16)


def inverse_x_tables(base, fine, kinds, blocks, width, scale):
    span = fine[0].shape[1]
    count = kinds.shape[0]

    def body(kinds_ref, blocks_ref, cos_ref, sin_ref, fine_cos, fine_sin, out_ref):
        first, second = pick(kinds_ref[pl.program_id(0)] > 0, cos_ref[...], sin_ref[...])
        fine_c, fine_s = fine_cos[...] * scale, fine_sin[...] * scale
        for a in range(width // STEP):
            lines = spread(first[a : a + 1], second[a : a + 1], fine_c, fine_s, 1.0)
            for j in range(span // TILE):
                out_ref[j, a * STEP : (a + 1) * STEP] = lines[:, j * TILE : (j + 1) * TILE]

    rows = pl.BlockSpec((width // STEP, span), lambda i, k, b: (b[i], 0))
    return call(
        body,
        jax.ShapeDtypeStruct((span // TILE, count * width, TILE), jnp.bfloat16),
        (count,),
        (*base, *fine),
        [rows, rows, whole((STEP, span)), whole((STEP, span))],
        pl.BlockSpec((span // TILE, width, TILE), lambda i, k, b: (0, i, 0)),
        4 * count * width * span,
        2 * count * width * span,
        "tables_ix",
        (kinds, blocks),
    )


def forward_y_tables(base, fine, member, members, share, modes):
    order = [member ^ s for s in range(members)]
    weight = (2.0 * math.sqrt(modes) / NY) * jnp.where(jnp.arange(base[0].shape[1]) == 0, 1.0, 2.0)[None]
    lines = (*base, *fine, weight)
    block = share
    if share % 128:
        lines = [
            jnp.concatenate([lax.dynamic_slice_in_dim(a, o * share, share, 1) for o in order], axis=1) for a in lines
        ]
        order, block = [jnp.zeros((), jnp.int32)], members * share

    def body(order_ref, cos_ref, sin_ref, fine_cos, fine_sin, weight_ref, out_ref):
        cosine = pl.program_id(0) == 0
        fine_c, fine_s, scale = fine_cos[...], fine_sin[...], weight_ref[...]
        for a in range(modes // STEP):
            first, second = pick(cosine, cos_ref[a : a + 1], sin_ref[a : a + 1])
            out_ref[a * STEP : (a + 1) * STEP] = spread(first, second, fine_c, fine_s, scale)

    def part(height):
        return pl.BlockSpec((height, block), lambda h, s, o: (0, o[s]))

    return call(
        body,
        jax.ShapeDtypeStruct((2 * modes, members * share), jnp.bfloat16),
        (2, len(order)),
        lines,
        [part(a.shape[0]) for a in lines],
        pl.BlockSpec((modes, block), lambda h, s, o: (h, s)),
        8 * modes * members * share,
        4 * modes * members * share,
        "tables_fy",
        (jnp.stack(order),),
    )


def forward_x_tables(base, fine, kinds, blocks, width, modes):
    steps = base[0].shape[0]
    count = kinds.shape[0]
    unit = 2.0 * math.sqrt(modes) / NX

    def body(kinds_ref, blocks_ref, cos_ref, sin_ref, fine_cos, fine_sin, out_ref):
        cosine = kinds_ref[pl.program_id(0)] > 0
        fine_c, fine_s = fine_cos[...], fine_sin[...]
        for a in range(steps):
            first, second = pick(cosine, cos_ref[a : a + 1], sin_ref[a : a + 1])
            scale = 2.0 * unit
            if a == 0 or (a + 1) * STEP > NX // 2:
                point = lax.broadcasted_iota(jnp.int32, (STEP, 1), 0) + a * STEP
                ends = (point == 0) | (point == NX // 2)
                scale = unit * jnp.where(ends, 1.0, jnp.where(point > NX // 2, 0.0, 2.0))
            out_ref[a * STEP : (a + 1) * STEP] = spread(first, second, fine_c, fine_s, scale)

    rows = pl.BlockSpec((steps, width), lambda i, k, b: (0, b[i]))
    thin = pl.BlockSpec((STEP, width), lambda i, k, b: (0, b[i]))
    return call(
        body,
        jax.ShapeDtypeStruct((steps * STEP, count * width), jnp.bfloat16),
        (count,),
        (*base, *fine),
        [rows, rows, thin, thin],
        pl.BlockSpec((steps * STEP, width), lambda i, k, b: (0, i)),
        4 * steps * STEP * count * width,
        2 * steps * STEP * count * width,
        "tables_fx",
        (kinds, blocks),
    )


def inverse_y_table(base, fine, member, share, modes):
    rows = 2 * share + EDGE
    scale = 1.0 / math.sqrt(modes)

    def body(member_ref, cos_ref, sin_ref, fine_cos, fine_sin, out_ref):
        start = member_ref[0] * (share // STEP)
        fine_c, fine_s = fine_cos[...], fine_sin[...]
        for a in range(share // STEP):
            base_cos, base_sin = cos_ref[pl.ds(start + a, 1)], sin_ref[pl.ds(start + a, 1)]
            out_ref[a * STEP : (a + 1) * STEP] = spread(base_cos, -base_sin, fine_c, fine_s, scale)
            low = share + EDGE + a * STEP
            out_ref[low : low + STEP] = spread(base_sin, base_cos, fine_c, fine_s, scale)
        edge = NY // 2 // STEP
        for a in range(EDGE // STEP):
            low = share + a * STEP
            out_ref[low : low + STEP] = spread(
                cos_ref[edge : edge + 1], -sin_ref[edge : edge + 1], fine_c, fine_s, scale
            )

    return call(
        body,
        jax.ShapeDtypeStruct((rows, modes), jnp.bfloat16),
        (1,),
        (*base, *fine),
        [whole(a.shape) for a in (*base, *fine)],
        whole((rows, modes)),
        4 * rows * modes,
        2 * rows * modes,
        "tables_iy",
        (member[None],),
    )


def inverse_y(table, piece, share):
    modes = table.shape[1]
    rows, width = table.shape[0], piece.shape[1]
    top, step = share + EDGE, rows // BLOCKS

    def body(*refs):
        even_ref, odd_ref, out_ref = refs[BLOCKS:]
        for j in range(BLOCKS):
            low = j * step
            cut = min(max(top - low, 0), step)
            if cut:
                out_ref[low : low + cut] = dot(refs[j][:cut], even_ref[...]).astype(jnp.bfloat16)
            if cut < step:
                out_ref[low + cut : low + step] = dot(refs[j][cut:], odd_ref[...]).astype(jnp.bfloat16)

    def part(shape, j):
        return pl.BlockSpec(shape, lambda i: (j, 0))

    return call(
        body,
        jax.ShapeDtypeStruct((rows, width), jnp.bfloat16),
        (1,),
        (*[table] * BLOCKS, piece, piece),
        [part((step, modes), j) for j in range(BLOCKS)] + [part((modes, width), j) for j in range(2)],
        whole((rows, width)),
        2 * rows * modes * width,
        2 * (rows * modes + 2 * modes * width + rows * width),
        "inverse_y",
    )


def inverse_x(lines, table, part):
    rows, width = lines[0].shape
    tiles = table.shape[0]
    count = len(lines)

    def body(*refs):
        table_ref, out_ref = refs[count], refs[count + 1]
        lines_here = jnp.concatenate([r[...] for r in refs[:count]], axis=1)
        out_ref[0] = dot(lines_here, table_ref[0]).astype(jnp.bfloat16)

    return call(
        body,
        jax.ShapeDtypeStruct((tiles, rows, TILE), jnp.bfloat16),
        (tiles,),
        (*lines, table),
        [whole((rows, width))] * count + [pl.BlockSpec((1, count * width, TILE), lambda i: (i, part, 0))],
        pl.BlockSpec((1, rows, TILE), lambda i: (i, 0, 0)),
        2 * rows * count * width * tiles * TILE,
        4 * rows * tiles * TILE,
        "inverse_x",
    )


def grid_term(lines, table, part, mine, table_back, turn, members, strength, sign, share):
    rows, width = lines[0].shape
    tiles = table.shape[0]
    count = len(lines)
    top = share + EDGE
    chunk = share // 2

    def body(*refs):
        strength_ref, sign_ref = refs[:2]
        line_refs = refs[2 : 2 + count]
        table_ref, mine_ref, back_ref, mine_out, other_out = refs[2 + count : 7 + count]
        out_refs, kept_ref = refs[7 + count : -1], refs[-1]
        c, s = strength_ref[0], sign_ref[0]
        step = pl.program_id(0)

        def other(*parts):
            picked = [jnp.concatenate([r[low : low + size] for low, size in parts], axis=0) for r in line_refs]
            return dot(jnp.concatenate(picked, axis=1), table_ref[0])

        def put(ref, low, value):
            ref[0, low : low + value.shape[0]] = value.astype(jnp.bfloat16)

        @pl.when(step < tiles)
        def _():
            for low in range(0, share, chunk):
                both = other((low, chunk), (top + low, chunk))
                x, y = both[:chunk], both[chunk:]
                a = mine_ref[0, low : low + chunk].astype(jnp.float32)
                b = mine_ref[0, top + low : top + low + chunk].astype(jnp.float32)
                p, q, u, v = a + x, b + y, a - x, b - y
                sums, gaps = (p * p + q * q) * (0.5 * c), (u * u + v * v) * (0.5 * c * s)
                cross, skew = (p * q) * c, (u * v) * (c * s)
                put(other_out, low, x + (sums - gaps))
                put(other_out, top + low, y + (cross - skew))
                put(mine_out, low, a + (sums + gaps))
                put(mine_out, top + low, b + (cross + skew))
            x, a = other((share, EDGE)), mine_ref[0, share:top].astype(jnp.float32)
            p, u = a + x, a - x
            sums, gaps = (p * p) * (0.5 * c), (u * u) * (0.5 * c * s)
            put(other_out, share, x + (sums - gaps))
            put(mine_out, share, a + (sums + gaps))
            kept_ref[step] = other_out[0]

        for j, out_ref in enumerate(out_refs):

            @pl.when(step == tiles + j)
            def _():
                points = jnp.concatenate([kept_ref[k] for k in range(tiles)], axis=1)
                out_ref[...] = dot(points, back_ref[...]).astype(jnp.bfloat16)

    def clip(i):
        return jnp.minimum(i, tiles - 1)

    def owner(i, *_):
        return (0, turn * members + lax.rem(jnp.clip(i - tiles, 0, members - 1) + 1, members))

    tile = pl.BlockSpec((1, rows, TILE), lambda i, *_: (clip(i), 0, 0))
    mine, other, *parts = call(
        body,
        [jax.ShapeDtypeStruct((tiles, rows, TILE), jnp.bfloat16)] * 2
        + [jax.ShapeDtypeStruct((rows, width), jnp.bfloat16)] * members,
        (tiles + members,),
        (*lines, table, mine, table_back),
        [whole((rows, width))] * count
        + [
            pl.BlockSpec((1, count * width, TILE), lambda i, *_: (clip(i), part, 0)),
            tile,
            pl.BlockSpec((tiles * TILE, width), owner),
        ],
        [tile, tile] + [whole((rows, width))] * members,
        2 * rows * (count + members) * width * tiles * TILE,
        8 * rows * tiles * TILE,
        "grid_term",
        (strength, sign),
        scratch=[pltpu.VMEM((tiles, rows, TILE), jnp.bfloat16)],
    )
    return mine, other, parts[-1:] + parts[:-1]


def forward_x(sources, table_back, pieces, width):
    tiles, rows = sources[0].shape[:2]
    count = len(sources)

    def body(*refs):
        table_ref, out_refs = refs[1 + tiles * count], refs[2 + tiles * count :]
        for j, (source, _) in enumerate(pieces):

            @pl.when(pl.program_id(0) == j)
            def _():
                first = 1 + source * tiles
                points = jnp.concatenate([refs[first + k][0] for k in range(tiles)], axis=1)
                out_refs[j][...] = dot(points, table_ref[...]).astype(jnp.bfloat16)

    def tile(k):
        return pl.BlockSpec((1, rows, TILE), lambda i, c: (k, 0, 0), pipeline_mode=pl.Buffered(1))

    return call(
        body,
        [jax.ShapeDtypeStruct((rows, width), jnp.bfloat16)] * len(pieces),
        (len(pieces),),
        (*[s for s in sources for _ in range(tiles)], table_back),
        [tile(k) for _ in sources for k in range(tiles)]
        + [pl.BlockSpec((tiles * TILE, width), lambda i, c: (0, c[i]))],
        [whole((rows, width))] * len(pieces),
        2 * rows * tiles * TILE * len(pieces) * width,
        2 * count * rows * tiles * TILE,
        "forward_x",
        (jnp.array([column for _, column in pieces], jnp.int32),),
    )


def forward_y(lines, table, column_start, slot, share, bounds, fields=0):
    width = lines[0].shape[1]
    modes = table.shape[0] // 2
    top = share + EDGE
    count = len(lines)

    def body(*refs):
        where_ref, table_refs = refs[0], refs[1 + count : 1 + count + BLOCKS]
        out_refs = refs[1 + count + BLOCKS :]
        half = pl.program_id(0)
        low = pl.multiple_of(half * top, STEP)
        points = jnp.concatenate([r[pl.ds(low, share)] for r in refs[1 : 1 + count]], axis=0)
        total = jnp.concatenate([dot(r[...], points) for r in table_refs], axis=0)
        waves = lax.broadcasted_iota(jnp.int32, (modes, 1), 0) + 1
        unit = jnp.where(half == 0, 2.0 * math.sqrt(modes) / NY, 0.0)
        nyquist = jnp.where(waves % 2 == 1, -unit, unit).astype(jnp.bfloat16).astype(jnp.float32)
        total += nyquist * refs[1][share : share + 1].astype(jnp.float32)
        across = lax.broadcasted_iota(jnp.int32, (1, width), 1) + where_ref[0] + 1
        inside = waves * waves <= modes * modes - across * across
        total = jnp.where(inside, total, 0.0).astype(jnp.bfloat16)
        if fields:
            out_refs[0][0] = total
        else:
            for out_ref, start, stop in zip(out_refs, bounds[:-1], bounds[1:]):
                out_ref[0] = total[start:stop]

    def fetch(j):
        return pl.BlockSpec((modes // BLOCKS, count * share), lambda i, s: (BLOCKS * i + j, 0))

    if fields:
        outs = jax.ShapeDtypeStruct((fields, 2 * modes, width), jnp.bfloat16)
        out_specs = pl.BlockSpec((1, modes, width), lambda i, s: (s[1], i, 0))
    else:
        sizes = [high - low for low, high in zip(bounds[:-1], bounds[1:])]
        outs = [jax.ShapeDtypeStruct((2, n, width), jnp.bfloat16) for n in sizes]
        out_specs = [pl.BlockSpec((1, n, width), lambda i, s: (i, 0, 0)) for n in sizes]
    return call(
        body,
        outs,
        (2,),
        (*lines, *[table] * BLOCKS),
        [whole(lines[0].shape)] * count + [fetch(j) for j in range(BLOCKS)],
        out_specs,
        4 * modes * share * count * width,
        2 * (2 * modes * share * count + 2 * modes * width),
        "forward_y",
        (jnp.stack([column_start, slot]),),
    )


def place(result, blocks, bounds, slot):
    _, height, width = result.shape
    modes = height // 2
    count = len(blocks)

    def body(*refs):
        out_ref = refs[-1]
        for j in range(count):
            out_ref[0, bounds[j] : bounds[j + 1]] = refs[1 + j][0]

    return call(
        body,
        jax.ShapeDtypeStruct(result.shape, result.dtype),
        (2,),
        (*blocks, result),
        [pl.BlockSpec((1, *b.shape[1:]), lambda i, s: (i, 0, 0)) for b in blocks] + [pl.BlockSpec(memory_space=pl.ANY)],
        pl.BlockSpec((1, modes, width), lambda i, s: (s[0], i, 0)),
        height * width,
        4 * height * width,
        "place",
        (slot[None],),
        input_output_aliases={1 + count: 0},
    )


def row_limits(modes, width, devices):
    limits = []
    for c in range(devices):
        low = (c * width) % modes + 1
        limits.append(min(modes, -(-math.isqrt(modes * modes - low * low) // 16) * 16))
    return limits


def round_trip(devices, spectra, coupling):
    fields, height, width = spectra.shape
    modes = height // 2
    members = devices // fields
    share = NY // 2 // members
    span = NX // 2 + TILE
    half = fields // 2
    me = lax.axis_index("col")
    group, member = me // members, me % members
    first_field = lax.axis_index("row") * fields
    strength = lax.dynamic_slice_in_dim(coupling, first_field + group, 1)
    is_mine = group < half
    sign = jnp.where(is_mine, 1.0, -1.0)[None]

    def send(piece, turn, shift, chosen=None):
        partners = []
        for c in range(devices):
            there = ((c // members) ^ turn) * members + ((c % members) ^ shift)
            if chosen is None or there in chosen:
                partners.append((c, there))
        return lax.ppermute(piece, "col", partners)

    pieces = [lax.dynamic_index_in_dim(spectra, group ^ t, 0, keepdims=False) for t in range(fields)]
    arrived = [pieces[0]] + [send(pieces[t], t, 0) for t in range(1, fields)]

    def ints(n, by=1):
        return jnp.arange(n, dtype=jnp.int32) * by

    by_mode = angle_pair(ints(modes // STEP, STEP) + 1, ints(span), NX) + angle_pair(ints(STEP), ints(span), NX)
    by_point = angle_pair(ints(span // STEP, STEP), ints(modes) + 1, NX) + angle_pair(ints(STEP), ints(modes) + 1, NX)
    by_mode, by_point = lax.optimization_barrier((by_mode, by_point))
    owners = jnp.stack([(group ^ t) * members + (member ^ s) for t in range(fields) for s in range(members)])
    kinds = (owners * width < modes).astype(jnp.int32)
    blocks = owners % (modes // width)
    table_y = inverse_y_table(by_point[:2], by_point[2:], member, share, modes)
    table_x = inverse_x_tables(by_mode[:2], by_mode[2:], kinds, blocks, width, 1.0 / math.sqrt(modes))
    table_back_x = forward_x_tables(by_point[:2], by_point[2:], kinds, blocks, width, modes)
    table_back_y = forward_y_tables(by_mode[:2], by_mode[2:], member, members, share, modes)

    lines = []
    for t in range(fields):
        for s in range(members):
            piece = arrived[t] if s == 0 else send(arrived[t], 0, s)
            lines.append(inverse_y(table_y, piece, share))
    cut = half * members
    mine = inverse_x(lines[:cut], table_x, 0)
    order = turns(fields)
    mine, other, parts = grid_term(
        lines[cut:], table_x, 1, mine, table_back_x, order[0], members, strength, sign, share
    )

    limits = row_limits(modes, width, devices)
    levels = sorted(set(limits))
    while len(levels) > LEVELS:
        gaps = [(levels[i + 1] - levels[i], i) for i in range(len(levels) - 1)]
        levels.pop(min(gaps)[1])
    bounds = [0] + levels
    bounds[-1] = modes

    returned, result, ready, batches = {}, None, {}, back_batches(fields)
    for t in order:
        for later in batches:
            if t == later[0]:
                kinds_here = sorted({u >= half for u in later})
                flat = forward_x(
                    [(mine, other)[k] for k in kinds_here],
                    table_back_x,
                    [(kinds_here.index(u >= half), u * members + s) for u in later for s in [*range(1, members), 0]],
                    width,
                )
                ready.update({u: flat[j * members : (j + 1) * members] for j, u in enumerate(later)})
        if t in ready:
            parts = ready[t][-1:] + ready[t][:-1]
        rows = [parts[0]] + [send(parts[s], 0, s) for s in range(1, members)]
        start = (((group ^ t) * members + member) * width) % modes
        cuts = bounds if t > 1 else [0, modes]
        sums = forward_y(rows, table_back_y, start, group, share, cuts, fields if t == 0 else 0)
        if t == 0:
            result = sums
        else:
            returned[t] = [
                send(b, t, 0, [c for c in range(devices) if limits[c] > cuts[j]])
                for j, b in enumerate(sums)
            ]
    for t, parts in returned.items():
        result = place(result, parts, bounds if t > 1 else [0, modes], group ^ t)
    return result


def turns(fields):
    return [fields - 1, *range(1, fields - 1), 0]


def back_batches(fields):
    return [turns(fields)[1:]]


def solution(mesh):
    placed = (P("row", None, "col"), P())
    devices = mesh.shape["col"]

    def body(spectra, coupling):
        return round_trip(devices, spectra, coupling)

    return jax.shard_map(body, mesh=mesh, in_specs=placed, out_specs=P("row", None, "col"), check_vma=False)
```

time: 506 us -> 315 us (0.62)
  waiting for transfers between devices: 278 us -> 99.2 us
  Pallas kernels: 0 us -> 127 us
  matrix products: 96.8 us -> 0 us
  local copies, waits for them, and re-layouts: 66.6 us -> 17.7 us
  starting transfers between devices: 11.1 us -> 56 us
  other arithmetic: 52.9 us -> 12.6 us
    all_to_all x2 -> x0, waiting for transfers between devices: 278 us -> none  [the longest x1 139 us: on_device(): lax.all_to_all(half_done, 'col', split_axis=1, concat_axis=2, tiled=True)]
    pallas_call x0 -> x22, Pallas kernels: none -> 127 us  [call(): pl.pallas_call(body, out_shape=outs, grid_spec=pltpu.PrefetchScalarGridSp...]
    ppermute x0 -> x18, waiting for transfers between devices: none -> 99.2 us  [send(): return lax.ppermute(piece, 'col', partners)]
    dot_general x4 -> x0, matrix products: 96.8 us -> none  [the longest x1 27.8 us: on_device(): jnp.einsum('fyk,kx->fyx', gathered, inverse_x, preferred_element_type=jnp...]
    ppermute x0 -> x18, starting transfers between devices: none -> 56 us  [send(): return lax.ppermute(piece, 'col', partners)]
    cos x1 -> x0, other arithmetic: 52.6 us -> none  [fourier_rows(): table = jnp.concatenate([jnp.cos(angles), jnp.sin(angles)], 0) * factor]
    all_to_all x4 -> x0, local copies, waits for them, and re-layouts: 39.1 us -> none  [the longest x2 19.6 us: on_device(): lax.all_to_all(projected, 'col', split_axis=2, concat_axis=1, tiled=True)]
    convert_element_type x3 -> x0, local copies, waits for them, and re-layouts: 27.4 us -> none  [the longest x1 10.7 us: on_device(): projected = jnp.einsum('fyx,xk->fyk', tendency, forward_x, preferred_elem...]
  transfers between devices with their start and end apart: 2 -> 18, of which waited for: 2 -> 3; matrix products, arithmetic and copies ran while one was open for 0% -> 4% of each run, Pallas kernels for 0% -> 27%
where the time goes in v1:
time: 315 us; the launch traced here: 313 us
  Pallas kernels  127 us (40%)
  waiting for transfers between devices  99.2 us (31%)
  starting transfers between devices  56 us (18%)
  local copies, waits for them, and re-layouts  17.7 us (6%)
  other arithmetic  12.6 us (4%)
    pallas_call x22, Pallas kernels, call(): pl.pallas_call(body, out_shape=outs, grid_spec=pltpu.PrefetchScalarGridSp...  127 us
    ppermute x18, waiting for transfers between devices, send(): return lax.ppermute(piece, 'col', partners)  99.2 us
    ppermute x18, starting transfers between devices, send(): return lax.ppermute(piece, 'col', partners)  56 us
    unnamed x28, local copies, waits for them, and re-layouts  13.1 us
    sin x4, other arithmetic, angle_pair(): return (jnp.cos(angles), jnp.sin(angles))  7.8 us
  transfers between devices with their start and end apart: 18, of which 3 were waited for; matrix products, arithmetic and copies ran while one was open for 4% of the time, Pallas kernels for 27%

profile of v1, /device:TPU:0, one launch (start us, length us, event | category | flops | bytes accessed | tf_op | source)
XLA Modules:
  0.0 313.3 jit_solution(4296221083492964255)
XLA Ops:
  0.0 3.8 %dynamic-slice_bitcast_fusion = (bf16[2048,256]{1,0:T(8,128)(2,1)S(1)}, bf16[2048,256]{1,0:T(8,128)(2,1)}, bf16[2048,256]{1,0:T(8,128)(2,1)S(1)}, bf16[2048,256]{1,0:T(8,128)(2,1)}) fusion(bf16[4,2048,256]{2,1,0:T(8,128)(2,1)} %param.3, s32[]{:T(128)S(6)} %select_n.109, s32[]{:T(128)S(6)} %select_n.106, s32[]{:T(128)S(6)} %select_n.105, s32[]{:T(128)S(6)} %select_n.108), kind=kLoop, calls=%fused_computation | loop fusion | bytes 8388624 | tf_op jit(solution)/shard_map/jit(dynamic_index_in_dim)/squeeze | solution.py:459
  3.8 3.1 collective-permute-start.5
  6.9 2.6 collective-permute-start
  9.5 2.9 fusion.10
  12.4 2.9 fusion.6
  15.2 1.2 fusion.18
  16.4 35.2 %collective-permute-done.5.refs_4_.refs_5_ = bf16[2048,256]{1,0:T(8,128)(2,1)} collective-permute-done((bf16[2048,256]{1,0:T(8,128)(2,1)S(1)}, bf16[2048,256]{1,0:T(8,128)(2,1)}, u32[]{:S(2)}, u32[]{:S(2)}) %collective-permute-start.5) | collective-permute-done | bytes 1048608 | tf_op jit(solution)/shard_map/ppermute | solution.py:457
  51.6 27.4 %collective-permute-done.refs_4_.refs_5_ = bf16[2048,256]{1,0:T(8,128)(2,1)} collective-permute-done((bf16[2048,256]{1,0:T(8,128)(2,1)S(1)}, bf16[2048,256]{1,0:T(8,128)(2,1)}, u32[]{:S(2)}, u32[]{:S(2)}) %collective-permute-start) | collective-permute-done | bytes 1048608 | tf_op jit(solution)/shard_map/ppermute | solution.py:457
  78.9 0.9 fusion.25
  80.0 4.0 %shard_map.37.refs_0_.refs_1_.refs_2_.refs_3_ = bf16[1600,1024]{1,0:T(8,128)(2,1)} custom-call(s32[1]{0:T(128)} %bitcast.4.member_ref, f32[112,1024]{1,0:T(8,128)} %get-tuple-element.29.cos_ref, f32[112,1024]{1,0:T(8,128)} %get-tuple-element.30.sin_ref, f32[16,1024]{1,0:T(8,128)} %get-tuple-element.31.fine_cos, f32[16,1024]{1,0:T(8,128)} %get-tuple-element.32.fine_sin), custom_call_target="tpu_custom_call" | custom-call | flops 6553600 | bytes 3276800 | tf_op jit(solution)/shard_map/pallas_call | solution.py:37
  85.5 1.9 copy-done
  87.4 2.3 shard_map.43.refs_0_
  89.7 0.9 copy-done.3
  91.2 8.8 %shard_map.48.refs_8_.refs_15_ = bf16[1792,2048]{1,0:T(8,128)(2,1)} custom-call(s32[8]{0:T(128)} %compare_convert_fusion.kinds_ref, s32[8]{0:T(128)} %and_select_fusion.blocks_ref, f32[112,1024]{1,0:T(8,128)} %get-tuple-element.29.cos_ref, f32[112,1024]{1,0:T(8,128)} %get-tuple-element.30.sin_ref, f32[16,1024]{1,0:T(8,128)} %get-tuple-element.31.fine_cos, ...), custom_call_target="tpu_custom_call" | custom-call | flops 14680064 | bytes 7340032 | tf_op jit(solution)/shard_map/pallas_call | solution.py:37
  100.0 8.8 %shard_map.42.refs_4_.refs_6_ = bf16[7,2048,256]{2,1,0:T(8,128)(2,1)} custom-call(s32[8]{0:T(128)} %compare_convert_fusion.kinds_ref, s32[8]{0:T(128)} %and_select_fusion.blocks_ref, f32[64,1792]{1,0:T(8,128)} %get-tuple-element.33.cos_ref, f32[64,1792]{1,0:T(8,128)} %get-tuple-element.34.sin_ref, f32[16,1792]{1,0:T(8,128)} %get-tuple-element.35.fine_cos, ...), custom_call_target="tpu_custom_call" | custom-call | flops 14680064 | bytes 7340032 | tf_op jit(solution)/shard_map/pallas_call | solution.py:37
  108.9 1.9 copy-done.1
  110.8 2.3 shard_map.45.refs_2_
  113.1 1.0 copy-done.7
  114.0 2.3 shard_map.40.refs_4_
  116.3 0.9 copy-done.4
  117.2 2.3 shard_map.38.refs_2_
  119.5 0.9 copy-done.5
  120.4 2.3 shard_map.44.refs_1_
  122.7 0.9 copy-done.8
  123.7 2.3 shard_map.46.refs_3_
  125.9 0.9 copy-done.10
  126.8 2.3 shard_map.39.refs_3_
  129.1 0.9 copy-done.6
  130.0 11.1 %shard_map.47.refs_7_ = bf16[7,1600,256]{2,1,0:T(8,128)(2,1)} custom-call(bf16[1600,256]{1,0:T(8,128)(2,1)} %copy-done.3, bf16[1600,256]{1,0:T(8,128)(2,1)} %copy-done.8, bf16[1600,256]{1,0:T(8,128)(2,1)} %copy-done.7, bf16[1600,256]{1,0:T(8,128)(2,1)} %copy-done.10, bf16[7,2048,256]{2,1,0:T(8,128)(2,1)} %shard_map.42.refs_4_.refs_6_), custom_call_target="tpu_custom_call" | custom-call | flops 5872025600 | bytes 11468800 | tf_op jit(solution)/shard_map/pallas_call | solution.py:37
  141.1 1.9 copy-done.2
  143.1 2.3 shard_map.41.refs_5_
  146.2 21.1 %shard_map.49 = (bf16[7,1600,256]{2,1,0:T(8,128)(2,1)}, bf16[7,1600,256]{2,1,0:T(8,128)(2,1)}, bf16[1600,256]{1,0:T(8,128)(2,1)}, bf16[1600,256]{1,0:T(8,128)(2,1)}) custom-call(f32[1]{0:T(128)} %dynamic_slice.16.refs_0_, f32[1]{0:T(128)} %bitcast.3.refs_1_, bf16[1600,256]{1,0:T(8,128)(2,1)} %copy-done.5, bf16[1600,256]{1,0:T(8,128)(2,1)} %copy-done.6, ...), custom_call_target="tpu_custom_call" | custom-call | flops 8808038400 | bytes 22937600 | tf_op jit(solution)/shard_map/pallas_call | solution.py:37
  167.3 18.0 %shard_map.50 = (bf16[1600,256]{1,0:T(8,128)(2,1)}, bf16[1600,256]{1,0:T(8,128)(2,1)}, bf16[1600,256]{1,0:T(8,128)(2,1)}, bf16[1600,256]{1,0:T(8,128)(2,1)}, bf1...) custom-call(s32[6]{0:T(128)} %constant.136.clone.refs_0_, ...), custom_call_target="tpu_custom_call" | custom-call | flops 8808038400 | bytes 11468800 | tf_op jit(solution)/shard_map/pallas_call | solution.py:37
  187.2 6.7 %shard_map.51.refs_3_.refs_4_.refs_5_.refs_6_ = bf16[2048,1536]{1,0:T(8,128)(2,1)} custom-call(s32[2]{0:T(128)} %pad_add_fusion.1.order_ref, f32[64,1792]{1,0:T(8,128)} %get-tuple-element.33.cos_ref, f32[64,1792]{1,0:T(8,128)} %get-tuple-element.34.sin_ref, f32[16,1792]{1,0:T(8,128)} %get-tuple-element.35.fine_cos, f32[16,1792]{1,0:T(8,128)} %get-tuple-element.36.fine_sin, ...), custom_call_target="tpu_custom_call" | custom-call | flops 12582912 | bytes 6291456 | tf_op jit(solution)/shard_map/pallas_call | solution.py:37
  195.6 6.2 %shard_map.53 = bf16[2,1024,256]{2,1,0:T(8,128)(2,1)} custom-call(s32[2]{0:T(128)} %pad_add_fusion.2.refs_0_, bf16[1600,256]{1,0:T(8,128)(2,1)} %get-tuple-element.44.refs_1_, bf16[1600,256]{1,0:T(8,128)(2,1)} %collective-permute-done.11.refs_2_, bf16[2048,1536]{1,0:T(8,128)(2,1)} %shard_map.51.refs_3_.refs_4_.refs_5_.refs_6_, ...), custom_call_target="tpu_custom_call" | custom-call | flops 1610612736 | bytes 7340032 | tf_op jit(solution)/shard_map/pallas_call | solution.py:37
  201.7 16.2 %collective-permute-start.12 = (bf16[2,1024,256]{2,1,0:T(8,128)(2,1)}, bf16[2,1024,256]{2,1,0:T(8,128)(2,1)}, u32[]{:S(2)}, u32[]{:S(2)}) collective-permute-start(bf16[2,1024,256]{2,1,0:T(8,128)(2,1)} %shard_map.53), channel_id=1, source_target_pairs={{0,2},{1,3},{2,0},{3,1},{4,6},{5,7},{6,4},{7,5},{8,10},{9,11},{10,... | collective-permute-start | bytes 3145736 | tf_op jit(solution)/shard_map/ppermute | solution.py:457
  218.5 6.1 %shard_map.54 = (bf16[2,688,256]{2,1,0:T(8,128)(2,1)}, bf16[2,208,256]{2,1,0:T(8,128)(2,1)}, bf16[2,128,256]{2,1,0:T(8,128)(2,1)}) custom-call(s32[2]{0:T(128)} %pad_add_fusion.3.refs_0_, bf16[1600,256]{1,0:T(8,128)(2,1)} %get-tuple-element.46.refs_1_, bf16[1600,256]{1,0:T(8,128)(2,1)} %collective-permute-done.13.refs_2_, ...), custom_call_target="tpu_custom_call" | custom-call | flops 1610612736 | bytes 7340032 | tf_op jit(solution)/shard_map/pallas_call | solution.py:37
  224.6 2.5 collective-permute-start.14
  227.2 6.2 %shard_map.52 = (bf16[2,688,256]{2,1,0:T(8,128)(2,1)}, bf16[2,208,256]{2,1,0:T(8,128)(2,1)}, bf16[2,128,256]{2,1,0:T(8,128)(2,1)}) custom-call(s32[2]{0:T(128)} %pad_add_fusion.refs_0_, bf16[1600,256]{1,0:T(8,128)(2,1)} %get-tuple-element.39.refs_1_, bf16[1600,256]{1,0:T(8,128)(2,1)} %collective-permute-done.7.refs_2_, ...), custom_call_target="tpu_custom_call" | custom-call | flops 1610612736 | bytes 7340032 | tf_op jit(solution)/shard_map/pallas_call | solution.py:37
  233.4 1.3 collective-permute-start.16
  234.7 6.4 %collective-permute-start.15 = (bf16[2,208,256]{2,1,0:T(8,128)(2,1)}, bf16[2,208,256]{2,1,0:T(8,128)(2,1)}, u32[]{:S(2)}, u32[]{:S(2)}) collective-permute-start(bf16[2,208,256]{2,1,0:T(8,128)(2,1)} %get-tuple-element.49), channel_id=1, source_target_pairs={{0,6},{2,4},{3,5},{4,2},{6,0},{7,1},{8,14},{10,12},{11,13},{12,10}... | collective-permute-start | bytes 638984 | tf_op jit(solution)/shard_map/ppermute | solution.py:457
  241.1 36.7 %collective-permute-done.16.refs_3_ = bf16[2,128,256]{2,1,0:T(8,128)(2,1)S(1)} collective-permute-done((bf16[2,128,256]{2,1,0:T(8,128)(2,1)}, bf16[2,128,256]{2,1,0:T(8,128)(2,1)S(1)}, u32[]{:S(2)}, u32[]{:S(2)}) %collective-permute-start.16) | collective-permute-done | bytes 131104 | tf_op jit(solution)/shard_map/ppermute | solution.py:457
  277.7 19.1 %collective-permute-start.9 = (bf16[2,208,256]{2,1,0:T(8,128)(2,1)}, bf16[2,208,256]{2,1,0:T(8,128)(2,1)}, u32[]{:S(2)}, u32[]{:S(2)}) collective-permute-start(bf16[2,208,256]{2,1,0:T(8,128)(2,1)} %get-tuple-element.42), channel_id=1, source_target_pairs={{0,4},{1,5},{2,6},{4,0},{5,1},{6,2},{8,12},{9,13},{10,14},{12,8},{... | collective-permute-start | bytes 638984 | tf_op jit(solution)/shard_map/ppermute | solution.py:457
  297.5 3.4 %collective-permute-start.10 = (bf16[2,128,256]{2,1,0:T(8,128)(2,1)}, bf16[2,128,256]{2,1,0:T(8,128)(2,1)}, u32[]{:S(2)}, u32[]{:S(2)}) collective-permute-start(bf16[2,128,256]{2,1,0:T(8,128)(2,1)} %get-tuple-element.43), channel_id=1, source_target_pairs={{0,4},{1,5},{4,0},{5,1},{8,12},{9,13},{12,8},{13,9},{16,20},{17,21... | collective-permute-start | bytes 393224 | tf_op jit(solution)/shard_map/ppermute | solution.py:457
  300.9 6.2 %shard_map.55.refs_4_ = bf16[4,2048,256]{2,1,0:T(8,128)(2,1)} custom-call(s32[2]{0:T(128)} %pad_add_fusion.4.refs_0_, bf16[1600,256]{1,0:T(8,128)(2,1)} %get-tuple-element.51.refs_1_, bf16[1600,256]{1,0:T(8,128)(2,1)} %copy-done.11, bf16[2048,1536]{1,0:T(8,128)(2,1)} %shard_map.51.refs_3_.refs_4_.refs_5_.refs_6_, ...), custom_call_target="tpu_custom_call" | custom-call | flops 1610612736 | bytes 7340032 | tf_op jit(solution)/shard_map/pallas_call | solution.py:37
  307.1 2.1 shard_map.56.refs_2_
  309.2 2.0 shard_map.57.refs_4_
  311.3 2.1 shard_map.58
  (56 shorter events, 8.0 us)
Async XLA Ops:
  3.8 47.7 %collective-permute-start.5 = (bf16[2048,256]{1,0:T(8,128)(2,1)S(1)}, bf16[2048,256]{1,0:T(8,128)(2,1)}, u32[]{:S(2)}, u32[]{:S(2)}) collective-permute-start(bf16[2048,256]{1,0:T(8,128)(2,1)S(1)} %get-tuple-element.53), channel_id=1, source_target_pairs={{0,2},{1,3},{2,0},{3,1},{4,6},{5,7},{6,4},{7,5},{8,10},{9,11},{10,... | collective-permute-start | bytes 3145736 | tf_op jit(solution)/shard_map/ppermute | solution.py:457
  6.9 113.5 %collective-permute-start.4 = (bf16[2048,256]{1,0:T(8,128)(2,1)}, bf16[2048,256]{1,0:T(8,128)(2,1)}, u32[]{:S(2)}, u32[]{:S(2)}) collective-permute-start(bf16[2048,256]{1,0:T(8,128)(2,1)} %get-tuple-element.56.refs_4_.refs_5_), channel_id=1, source_target_pairs={{0,1},{1,0},{2,3},{3,2},{4,5},{5,4},{6,7},{7,6},{8,9},{9,8},{10,11... | collective-permute-start | bytes 3145736 | tf_op jit(solution)/shard_map/ppermute | solution.py:457
  6.9 72.0 %collective-permute-start = (bf16[2048,256]{1,0:T(8,128)(2,1)S(1)}, bf16[2048,256]{1,0:T(8,128)(2,1)}, u32[]{:S(2)}, u32[]{:S(2)}) collective-permute-start(bf16[2048,256]{1,0:T(8,128)(2,1)S(1)} %get-tuple-element.55), channel_id=1, source_target_pairs={{0,4},{1,5},{2,6},{3,7},{4,0},{5,1},{6,2},{7,3},{8,12},{9,13},{10,... | collective-permute-start | bytes 3145736 | tf_op jit(solution)/shard_map/ppermute | solution.py:457
  9.5 75.5 %collective-permute-start.2 = (bf16[2048,256]{1,0:T(8,128)(2,1)}, bf16[2048,256]{1,0:T(8,128)(2,1)}, u32[]{:S(2)}, u32[]{:S(2)}) collective-permute-start(bf16[2048,256]{1,0:T(8,128)(2,1)} %get-tuple-element.54), channel_id=1, source_target_pairs={{0,6},{1,7},{2,4},{3,5},{4,2},{5,3},{6,0},{7,1},{8,14},{9,15},{10,... | collective-permute-start | bytes 3145736 | tf_op jit(solution)/shard_map/ppermute | solution.py:457
  51.6 72.1 %collective-permute-start.6 = (bf16[2048,256]{1,0:T(8,128)(2,1)}, bf16[2048,256]{1,0:T(8,128)(2,1)}, u32[]{:S(2)}, u32[]{:S(2)}) collective-permute-start(bf16[2048,256]{1,0:T(8,128)(2,1)} %collective-permute-done.5.refs_4_.refs_5_), channel_id=1, source_target_pairs={{0,1},{1,0},{2,3},{3,2},{4,5},{5,4},{6,7},{7,6},{8,9},{9,8},{10,11... | collective-permute-start | bytes 3145736 | tf_op jit(solution)/shard_map/ppermute | solution.py:457
  78.9 47.9 %collective-permute-start.1 = (bf16[2048,256]{1,0:T(8,128)(2,1)}, bf16[2048,256]{1,0:T(8,128)(2,1)}, u32[]{:S(2)}, u32[]{:S(2)}) collective-permute-start(bf16[2048,256]{1,0:T(8,128)(2,1)} %collective-permute-done.refs_4_.refs_5_), channel_id=1, source_target_pairs={{0,1},{1,0},{2,3},{3,2},{4,5},{5,4},{6,7},{7,6},{8,9},{9,8},{10,11... | collective-permute-start | bytes 3145736 | tf_op jit(solution)/shard_map/ppermute | solution.py:457
  84.5 6.1 %copy-start.13 = (f32[16]{0:T(128)S(1)}, f32[16]{0:T(128)}, u32[]{:S(2)}) copy-start(f32[16]{0:T(128)} %param.4) | copy-start | bytes 196
  85.0 56.2 %collective-permute-start.3 = (bf16[2048,256]{1,0:T(8,128)(2,1)}, bf16[2048,256]{1,0:T(8,128)(2,1)}, u32[]{:S(2)}, u32[]{:S(2)}) collective-permute-start(bf16[2048,256]{1,0:T(8,128)(2,1)} %collective-permute-done.2.refs_4_.refs_5_), channel_id=1, source_target_pairs={{0,1},{1,0},{2,3},{3,2},{4,5},{5,4},{6,7},{7,6},{8,9},{9,8},{10,11... | collective-permute-start | bytes 3145736 | tf_op jit(solution)/shard_map/ppermute | solution.py:457
  85.5 1.9 copy-start
  89.7 0.9 copy-start.3
  108.9 1.9 copy-start.1
  113.1 1.0 copy-start.7
  116.3 0.9 copy-start.4
  119.5 0.9 copy-start.5
  122.7 0.9 copy-start.8
  125.9 0.9 copy-start.10
  129.1 0.9 copy-start.6
  141.1 1.9 copy-start.2
  145.3 0.9 copy-start.9
  185.3 10.2 %collective-permute-start.11 = (bf16[1600,256]{1,0:T(8,128)(2,1)}, bf16[1600,256]{1,0:T(8,128)(2,1)}, u32[]{:S(2)}, u32[]{:S(2)}) collective-permute-start(bf16[1600,256]{1,0:T(8,128)(2,1)} %get-tuple-element.45), channel_id=1, source_target_pairs={{0,1},{1,0},{2,3},{3,2},{4,5},{5,4},{6,7},{7,6},{8,9},{9,8},{10,11... | collective-permute-start | bytes 2457608 | tf_op jit(solution)/shard_map/ppermute | solution.py:457
  185.4 33.1 %collective-permute-start.13 = (bf16[1600,256]{1,0:T(8,128)(2,1)}, bf16[1600,256]{1,0:T(8,128)(2,1)}, u32[]{:S(2)}, u32[]{:S(2)}) collective-permute-start(bf16[1600,256]{1,0:T(8,128)(2,1)} %get-tuple-element.47), channel_id=1, source_target_pairs={{0,1},{1,0},{2,3},{3,2},{4,5},{5,4},{6,7},{7,6},{8,9},{9,8},{10,11... | collective-permute-start | bytes 2457608 | tf_op jit(solution)/shard_map/ppermute | solution.py:457
  186.5 40.6 %collective-permute-start.7 = (bf16[1600,256]{1,0:T(8,128)(2,1)}, bf16[1600,256]{1,0:T(8,128)(2,1)}, u32[]{:S(2)}, u32[]{:S(2)}) collective-permute-start(bf16[1600,256]{1,0:T(8,128)(2,1)} %get-tuple-element.40), channel_id=1, source_target_pairs={{0,1},{1,0},{2,3},{3,2},{4,5},{5,4},{6,7},{7,6},{8,9},{9,8},{10,11... | collective-permute-start | bytes 2457608 | tf_op jit(solution)/shard_map/ppermute | solution.py:457
  195.2 39.5 %collective-permute-start.17 = (bf16[1600,256]{1,0:T(8,128)(2,1)}, bf16[1600,256]{1,0:T(8,128)(2,1)S(1)}, u32[]{:S(2)}, u32[]{:S(2)}) collective-permute-start(bf16[1600,256]{1,0:T(8,128)(2,1)} %get-tuple-element.52), channel_id=1, source_target_pairs={{0,1},{1,0},{2,3},{3,2},{4,5},{5,4},{6,7},{7,6},{8,9},{9,8},{10,11... | collective-permute-start | bytes 2457608 | tf_op jit(solution)/shard_map/ppermute | solution.py:457
  201.7 107.4 %collective-permute-start.12 = (bf16[2,1024,256]{2,1,0:T(8,128)(2,1)}, bf16[2,1024,256]{2,1,0:T(8,128)(2,1)}, u32[]{:S(2)}, u32[]{:S(2)}) collective-permute-start(bf16[2,1024,256]{2,1,0:T(8,128)(2,1)} %shard_map.53), channel_id=1, source_target_pairs={{0,2},{1,3},{2,0},{3,1},{4,6},{5,7},{6,4},{7,5},{8,10},{9,11},{10,... | collective-permute-start | bytes 3145736 | tf_op jit(solution)/shard_map/ppermute | solution.py:457
  224.6 82.5 %collective-permute-start.14 = (bf16[2,688,256]{2,1,0:T(8,128)(2,1)}, bf16[2,688,256]{2,1,0:T(8,128)(2,1)}, u32[]{:S(2)}, u32[]{:S(2)}) collective-permute-start(bf16[2,688,256]{2,1,0:T(8,128)(2,1)} %get-tuple-element.48), channel_id=1, source_target_pairs={{0,6},{1,7},{2,4},{3,5},{4,2},{5,3},{6,0},{7,1},{8,14},{9,15},{10,... | collective-permute-start | bytes 2113544 | tf_op jit(solution)/shard_map/ppermute | solution.py:457
  233.4 77.9 %collective-permute-start.8 = (bf16[2,688,256]{2,1,0:T(8,128)(2,1)}, bf16[2,688,256]{2,1,0:T(8,128)(2,1)}, u32[]{:S(2)}, u32[]{:S(2)}) collective-permute-start(bf16[2,688,256]{2,1,0:T(8,128)(2,1)} %get-tuple-element.41), channel_id=1, source_target_pairs={{0,4},{1,5},{2,6},{3,7},{4,0},{5,1},{6,2},{7,3},{8,12},{9,13},{10,... | collective-permute-start | bytes 2113544 | tf_op jit(solution)/shard_map/ppermute | solution.py:457
  233.4 44.4 %collective-permute-start.16 = (bf16[2,128,256]{2,1,0:T(8,128)(2,1)}, bf16[2,128,256]{2,1,0:T(8,128)(2,1)S(1)}, u32[]{:S(2)}, u32[]{:S(2)}) collective-permute-start(bf16[2,128,256]{2,1,0:T(8,128)(2,1)} %get-tuple-element.50), channel_id=1, source_target_pairs={{2,4},{3,5},{6,0},{7,1},{10,12},{11,13},{14,8},{15,9},{18,20},{19,... | collective-permute-start | bytes 393224 | tf_op jit(solution)/shard_map/ppermute | solution.py:457
  234.7 66.3 %copy-start.11 = (bf16[1600,256]{1,0:T(8,128)(2,1)}, bf16[1600,256]{1,0:T(8,128)(2,1)S(1)}, u32[]{:S(2)}) copy-start(bf16[1600,256]{1,0:T(8,128)(2,1)S(1)} %collective-permute-done.17.refs_2_) | copy-start | bytes 2457604
  234.7 62.8 %collective-permute-start.15 = (bf16[2,208,256]{2,1,0:T(8,128)(2,1)}, bf16[2,208,256]{2,1,0:T(8,128)(2,1)}, u32[]{:S(2)}, u32[]{:S(2)}) collective-permute-start(bf16[2,208,256]{2,1,0:T(8,128)(2,1)} %get-tuple-element.49), channel_id=1, source_target_pairs={{0,6},{2,4},{3,5},{4,2},{6,0},{7,1},{8,14},{10,12},{11,13},{12,10}... | collective-permute-start | bytes 638984 | tf_op jit(solution)/shard_map/ppermute | solution.py:457
  277.7 29.4 %copy-start.12 = (bf16[2,128,256]{2,1,0:T(8,128)(2,1)}, bf16[2,128,256]{2,1,0:T(8,128)(2,1)S(1)}, u32[]{:S(2)}) copy-start(bf16[2,128,256]{2,1,0:T(8,128)(2,1)S(1)} %collective-permute-done.16.refs_3_) | copy-start | bytes 393220
  277.7 33.5 %collective-permute-start.9 = (bf16[2,208,256]{2,1,0:T(8,128)(2,1)}, bf16[2,208,256]{2,1,0:T(8,128)(2,1)}, u32[]{:S(2)}, u32[]{:S(2)}) collective-permute-start(bf16[2,208,256]{2,1,0:T(8,128)(2,1)} %get-tuple-element.42), channel_id=1, source_target_pairs={{0,4},{1,5},{2,6},{4,0},{5,1},{6,2},{8,12},{9,13},{10,14},{12,8},{... | collective-permute-start | bytes 638984 | tf_op jit(solution)/shard_map/ppermute | solution.py:457
  297.5 13.7 %collective-permute-start.10 = (bf16[2,128,256]{2,1,0:T(8,128)(2,1)}, bf16[2,128,256]{2,1,0:T(8,128)(2,1)}, u32[]{:S(2)}, u32[]{:S(2)}) collective-permute-start(bf16[2,128,256]{2,1,0:T(8,128)(2,1)} %get-tuple-element.43), channel_id=1, source_target_pairs={{0,4},{1,5},{4,0},{5,1},{8,12},{9,13},{12,8},{13,9},{16,20},{17,21... | collective-permute-start | bytes 393224 | tf_op jit(solution)/shard_map/ppermute | solution.py:457

commit v2 on v1

--- a/solution.py
+++ b/solution.py
@@ -240,19 +240,19 @@
     )
 
 
-def grid_term(lines, table, part, mine, table_back, turn, members, strength, sign, share):
+def grid_term(lines, table, part, mine, table_back, turn, members, strength, own_field, sign, share):
     rows, width = lines[0].shape
     tiles = table.shape[0]
     count = len(lines)
     top = share + EDGE
-    chunk = share // 2
+    chunk = share // 4
 
     def body(*refs):
-        strength_ref, sign_ref = refs[:2]
-        line_refs = refs[2 : 2 + count]
-        table_ref, mine_ref, back_ref, mine_out, other_out = refs[2 + count : 7 + count]
-        out_refs, kept_ref = refs[7 + count : -1], refs[-1]
-        c, s = strength_ref[0], sign_ref[0]
+        strength_ref, field_ref, sign_ref = refs[:3]
+        line_refs = refs[3 : 3 + count]
+        table_ref, mine_ref, back_ref, mine_out, other_out = refs[3 + count : 8 + count]
+        out_refs, kept_ref = refs[8 + count : -1], refs[-1]
+        c, s = strength_ref[field_ref[0]], sign_ref[0]
         step = pl.program_id(0)
 
         def other(*parts):
@@ -313,41 +313,46 @@
         2 * rows * (count + members) * width * tiles * TILE,
         8 * rows * tiles * TILE,
         "grid_term",
-        (strength, sign),
+        (strength, own_field, sign),
         scratch=[pltpu.VMEM((tiles, rows, TILE), jnp.bfloat16)],
     )
     return mine, other, parts[-1:] + parts[:-1]
 
 
-def forward_x(sources, table_back, pieces, width):
+def forward_x(sources, table_back, owners, members, width):
     tiles, rows = sources[0].shape[:2]
-    count = len(sources)
+    count, span = len(sources), members * width
 
     def body(*refs):
-        table_ref, out_refs = refs[1 + tiles * count], refs[2 + tiles * count :]
-        for j, (source, _) in enumerate(pieces):
-
-            @pl.when(pl.program_id(0) == j)
-            def _():
-                first = 1 + source * tiles
-                points = jnp.concatenate([refs[first + k][0] for k in range(tiles)], axis=1)
-                out_refs[j][...] = dot(points, table_ref[...]).astype(jnp.bfloat16)
-
-    def tile(k):
-        return pl.BlockSpec((1, rows, TILE), lambda i, c: (k, 0, 0), pipeline_mode=pl.Buffered(1))
-
-    return call(
-        body,
-        [jax.ShapeDtypeStruct((rows, width), jnp.bfloat16)] * len(pieces),
-        (len(pieces),),
-        (*[s for s in sources for _ in range(tiles)], table_back),
-        [tile(k) for _ in sources for k in range(tiles)]
-        + [pl.BlockSpec((tiles * TILE, width), lambda i, c: (0, c[i]))],
-        [whole((rows, width))] * len(pieces),
-        2 * rows * tiles * TILE * len(pieces) * width,
+        table_refs = refs[count : count + len(owners)]
+        out_refs, total_ref = refs[count + len(owners) : -1], refs[-1]
+
+        @pl.when(pl.program_id(0) == 0)
+        def _():
+            total_ref[...] = jnp.zeros_like(total_ref)
+
+        for j, (source, _) in enumerate(owners):
+            total_ref[:, j * span : (j + 1) * span] += dot(refs[source][0], table_refs[j][...])
+
+        @pl.when(pl.program_id(0) == tiles - 1)
+        def _():
+            for j, out_ref in enumerate(out_refs):
+                out_ref[...] = total_ref[:, j * width : (j + 1) * width].astype(jnp.bfloat16)
+
+    def columns(turn):
+        return pl.BlockSpec((TILE, span), lambda i: (i, turn))
+
+    return call(
+        body,
+        [jax.ShapeDtypeStruct((rows, width), jnp.bfloat16)] * (len(owners) * members),
+        (tiles,),
+        (*sources, *[table_back] * len(owners)),
+        [pl.BlockSpec((1, rows, TILE), lambda i: (i, 0, 0))] * count + [columns(turn) for _, turn in owners],
+        [whole((rows, width))] * (len(owners) * members),
+        2 * rows * tiles * TILE * len(owners) * span,
         2 * count * rows * tiles * TILE,
         "forward_x",
-        (jnp.array([column for _, column in pieces], jnp.int32),),
+        scratch=[pltpu.VMEM((rows, len(owners) * span), jnp.float32)],
     )
 
 
@@ -444,7 +449,7 @@
     me = lax.axis_index("col")
     group, member = me // members, me % members
     first_field = lax.axis_index("row") * fields
-    strength = lax.dynamic_slice_in_dim(coupling, first_field + group, 1)
+    own_field = (first_field + group)[None]
     is_mine = group < half
     sign = jnp.where(is_mine, 1.0, -1.0)[None]
 
@@ -456,7 +461,11 @@
                 partners.append((c, there))
         return lax.ppermute(piece, "col", partners)
 
-    pieces = [lax.dynamic_index_in_dim(spectra, group ^ t, 0, keepdims=False) for t in range(fields)]
+    first = lax.dynamic_index_in_dim(spectra, group ^ half, 0, keepdims=False)
+    first, spectra = lax.optimization_barrier((first, spectra))
+    pieces = [
+        first if t == half else lax.dynamic_index_in_dim(spectra, group ^ t, 0, keepdims=False) for t in range(fields)
+    ]
     arrived = [pieces[0]] + [send(pieces[t], t, 0) for t in range(1, fields)]
 
     def ints(n, by=1):
@@ -482,7 +491,7 @@
     mine = inverse_x(lines[:cut], table_x, 0)
     order = turns(fields)
     mine, other, parts = grid_term(
-        lines[cut:], table_x, 1, mine, table_back_x, order[0], members, strength, sign, share
+        lines[cut:], table_x, 1, mine, table_back_x, order[0], members, coupling, own_field, sign, share
     )
 
     limits = row_limits(modes, width, devices)
@@ -501,12 +510,13 @@
                 flat = forward_x(
                     [(mine, other)[k] for k in kinds_here],
                     table_back_x,
-                    [(kinds_here.index(u >= half), u * members + s) for u in later for s in [*range(1, members), 0]],
+                    [(kinds_here.index(u >= half), u) for u in later],
+                    members,
                     width,
                 )
                 ready.update({u: flat[j * members : (j + 1) * members] for j, u in enumerate(later)})
         if t in ready:
-            parts = ready[t][-1:] + ready[t][:-1]
+            parts = ready[t]
         rows = [parts[0]] + [send(parts[s], 0, s) for s in range(1, members)]
         start = (((group ^ t) * members + member) * width) % modes
         cuts = bounds if t > 1 else [0, modes]
@@ -528,7 +538,7 @@
 
 
 def back_batches(fields):
-    return [turns(fields)[1:]]
+    return [b for b in (turns(fields)[1:-1], [0]) if b]
 
 
 def solution(mesh):

time: 315 us -> 322 us (1.022)
  waiting for transfers between devices: 99.2 us -> 113 us
  starting transfers between devices: 56 us -> 43.1 us
  Pallas kernels: 127 us -> 131 us
    ppermute x18, waiting for transfers between devices: 99.2 us -> 113 us  [send(): return lax.ppermute(piece, 'col', partners)]
    ppermute x18, starting transfers between devices: 56 us -> 43.1 us  [send(): return lax.ppermute(piece, 'col', partners)]
    pallas_call x22 -> x23, Pallas kernels: 127 us -> 131 us  [call(): pl.pallas_call(body, out_shape=outs, grid_spec=pltpu.PrefetchScalarGridSp...]
    unnamed x28 -> x30, local copies, waits for them, and re-layouts: 13.1 us -> 14.7 us
  transfers between devices with their start and end apart: 18 -> 18, of which waited for: 3 -> 4; matrix products, arithmetic and copies ran while one was open for 4% -> 4% of each run, Pallas kernels for 27% -> 29%
where the time goes in v2:
time: 322 us; the launch traced here: 320 us
  Pallas kernels  131 us (41%)
  waiting for transfers between devices  113 us (35%)
  starting transfers between devices  43.1 us (13%)
  local copies, waits for them, and re-layouts  20.1 us (6%)
  other arithmetic  12.7 us (4%)
    pallas_call x23, Pallas kernels, call(): pl.pallas_call(body, out_shape=outs, grid_spec=pltpu.PrefetchScalarGridSp...  131 us
    ppermute x18, waiting for transfers between devices, send(): return lax.ppermute(piece, 'col', partners)  113 us
    ppermute x18, starting transfers between devices, send(): return lax.ppermute(piece, 'col', partners)  43.1 us
    unnamed x30, local copies, waits for them, and re-layouts  14.7 us
    sin x4, other arithmetic, angle_pair(): return (jnp.cos(angles), jnp.sin(angles))  7.78 us
  transfers between devices with their start and end apart: 18, of which 4 were waited for; matrix products, arithmetic and copies ran while one was open for 4% of the time, Pallas kernels for 29%

profile of v2, /device:TPU:0, one launch (start us, length us, event | category | flops | bytes accessed | tf_op | source)
XLA Modules:
  0.0 320.1 jit_solution(4206435676236479213)
XLA Ops:
  0.0 2.3 dynamic-slice_bitcast_fusion.3
  2.3 3.0 dynamic-slice_bitcast_fusion
  5.3 3.1 collective-permute-start.5
  8.4 2.5 collective-permute-start.2
  11.0 2.9 fusion.10
  13.8 2.8 fusion.6
  16.6 1.2 fusion.18
  17.8 14.1 %collective-permute-done.5.refs_4_.refs_5_ = bf16[2048,256]{1,0:T(8,128)(2,1)} collective-permute-done((bf16[2048,256]{1,0:T(8,128)(2,1)S(1)}, bf16[2048,256]{1,0:T(8,128)(2,1)}, u32[]{:S(2)}, u32[]{:S(2)}) %collective-permute-start.5) | collective-permute-done | bytes 1048608 | tf_op jit(solution)/shard_map/ppermute | solution.py:462
  31.9 25.6 %collective-permute-done.2.refs_4_.refs_5_ = bf16[2048,256]{1,0:T(8,128)(2,1)} collective-permute-done((bf16[2048,256]{1,0:T(8,128)(2,1)S(1)}, bf16[2048,256]{1,0:T(8,128)(2,1)}, u32[]{:S(2)}, u32[]{:S(2)}) %collective-permute-start.2) | collective-permute-done | bytes 1048608 | tf_op jit(solution)/shard_map/ppermute | solution.py:462
  57.5 0.9 fusion.25
  58.6 4.0 %shard_map.28.refs_0_.refs_1_.refs_2_.refs_3_ = bf16[1600,1024]{1,0:T(8,128)(2,1)} custom-call(s32[1]{0:T(128)} %bitcast.5.member_ref, f32[112,1024]{1,0:T(8,128)} %get-tuple-element.31.cos_ref, f32[112,1024]{1,0:T(8,128)} %get-tuple-element.32.sin_ref, f32[16,1024]{1,0:T(8,128)} %get-tuple-element.33.fine_cos, f32[16,1024]{1,0:T(8,128)} %get-tuple-element.34.fine_sin), custom_call_target="tpu_custom_call" | custom-call | flops 6553600 | bytes 3276800 | tf_op jit(solution)/shard_map/pallas_call | solution.py:37
  63.6 38.7 %collective-permute-done.refs_4_.refs_5_ = bf16[2048,256]{1,0:T(8,128)(2,1)} collective-permute-done((bf16[2048,256]{1,0:T(8,128)(2,1)}, bf16[2048,256]{1,0:T(8,128)(2,1)}, u32[]{:S(2)}, u32[]{:S(2)}) %collective-permute-start) | collective-permute-done | bytes 1048608 | tf_op jit(solution)/shard_map/ppermute | solution.py:462
  102.3 1.9 copy-done
  104.2 2.3 shard_map.34.refs_0_
  107.4 8.8 %shard_map.39.refs_9_.refs_2_.refs_3_.refs_1_ = bf16[1792,2048]{1,0:T(8,128)(2,1)} custom-call(s32[8]{0:T(128)} %compare_convert_fusion.kinds_ref, s32[8]{0:T(128)} %and_select_fusion.blocks_ref, f32[112,1024]{1,0:T(8,128)} %get-tuple-element.31.cos_ref, f32[112,1024]{1,0:T(8,128)} %get-tuple-element.32.sin_ref, f32[16,1024]{1,0:T(8,128)} %get-tuple-element.33.fine_cos, ...), custom_call_target="tpu_custom_call" | custom-call | flops 14680064 | bytes 7340032 | tf_op jit(solution)/shard_map/pallas_call | solution.py:37
  116.2 8.9 %shard_map.33.refs_4_.refs_7_ = bf16[7,2048,256]{2,1,0:T(8,128)(2,1)} custom-call(s32[8]{0:T(128)} %compare_convert_fusion.kinds_ref, s32[8]{0:T(128)} %and_select_fusion.blocks_ref, f32[64,1792]{1,0:T(8,128)} %get-tuple-element.37.cos_ref, f32[64,1792]{1,0:T(8,128)} %get-tuple-element.38.sin_ref, f32[16,1792]{1,0:T(8,128)} %get-tuple-element.39.fine_cos, ...), custom_call_target="tpu_custom_call" | custom-call | flops 14680064 | bytes 7340032 | tf_op jit(solution)/shard_map/pallas_call | solution.py:37
  125.1 1.9 copy-done.1
  127.0 2.3 shard_map.36.refs_2_
  129.3 0.9 copy-done.7
  130.2 2.3 shard_map.31.refs_5_
  132.5 0.9 copy-done.4
  133.4 2.3 shard_map.29.refs_3_
  135.7 0.9 copy-done.5
  136.6 2.3 shard_map.35.refs_1_
  139.7 2.3 shard_map.37.refs_3_
  142.0 0.9 copy-done.10
  142.9 2.3 shard_map.32.refs_6_
  145.2 0.9 copy-done.6
  146.1 11.1 %shard_map.38.refs_8_ = bf16[7,1600,256]{2,1,0:T(8,128)(2,1)} custom-call(bf16[1600,256]{1,0:T(8,128)(2,1)} %copy-done.3, bf16[1600,256]{1,0:T(8,128)(2,1)} %copy-done.8, bf16[1600,256]{1,0:T(8,128)(2,1)} %copy-done.7, bf16[1600,256]{1,0:T(8,128)(2,1)} %copy-done.10, bf16[7,2048,256]{2,1,0:T(8,128)(2,1)} %shard_map.33.refs_4_.refs_7_), custom_call_target="tpu_custom_call" | custom-call | flops 5872025600 | bytes 11468800 | tf_op jit(solution)/shard_map/pallas_call | solution.py:37
  157.2 1.9 copy-done.2
  159.1 2.3 shard_map.30.refs_4_
  162.3 20.5 %shard_map.40 = (bf16[7,1600,256]{2,1,0:T(8,128)(2,1)}, bf16[7,1600,256]{2,1,0:T(8,128)(2,1)}, bf16[1600,256]{1,0:T(8,128)(2,1)}, bf16[1600,256]{1,0:T(8,128)(2,1)}) custom-call(f32[16]{0:T(128)} %refs_0_.1, s32[1]{0:T(128)} %bitcast.3.refs_1_, f32[1]{0:T(128)} %bitcast.4.refs_2_, bf16[1600,256]{1,0:T(8,128)(2,1)} %copy-done.5, bf16[1600,256]{1,0:T(8,128)(2,1)} %copy-done.9, ...), custom_call_target="tpu_custom_call" | custom-call | flops 8808038400 | bytes 22937600 | tf_op jit(solution)/shard_map/pallas_call | solution.py:37
  182.9 12.9 %shard_map.41 = (bf16[1600,256]{1,0:T(8,128)(2,1)}, bf16[1600,256]{1,0:T(8,128)(2,1)}, bf16[1600,256]{1,0:T(8,128)(2,1)}, bf16[1600,256]{1,0:T(8,128)(2,1)}) custom-call(bf16[7,1600,256]{2,1,0:T(8,128)(2,1)} %get-tuple-element.41.refs_0_, bf16[7,1600,256]{2,1,0:T(8,128)(2,1)} %get-tuple-element.42.refs_1_, ...), custom_call_target="tpu_custom_call" | custom-call | flops 5872025600 | bytes 11468800 | tf_op jit(solution)/shard_map/pallas_call | solution.py:37
  198.7 6.6 %shard_map.42.refs_3_.refs_4_.refs_5_.refs_6_ = bf16[2048,1536]{1,0:T(8,128)(2,1)} custom-call(s32[2]{0:T(128)} %pad_add_fusion.1.order_ref, f32[64,1792]{1,0:T(8,128)} %get-tuple-element.37.cos_ref, f32[64,1792]{1,0:T(8,128)} %get-tuple-element.38.sin_ref, f32[16,1792]{1,0:T(8,128)} %get-tuple-element.39.fine_cos, f32[16,1792]{1,0:T(8,128)} %get-tuple-element.40.fine_sin, ...), custom_call_target="tpu_custom_call" | custom-call | flops 12582912 | bytes 6291456 | tf_op jit(solution)/shard_map/pallas_call | solution.py:37
  205.9 8.9 %shard_map.46 = (bf16[1600,256]{1,0:T(8,128)(2,1)}, bf16[1600,256]{1,0:T(8,128)(2,1)}) custom-call(bf16[7,1600,256]{2,1,0:T(8,128)(2,1)} %get-tuple-element.41.refs_0_, bf16[1792,2048]{1,0:T(8,128)(2,1)} %shard_map.39.refs_9_.refs_2_.refs_3_.refs_1_), custom_call_target="tpu_custom_call" | custom-call | flops 2936012800 | bytes 5734400 | tf_op jit(solution)/shard_map/pallas_call | solution.py:37
  214.8 6.2 %shard_map.44 = bf16[2,1024,256]{2,1,0:T(8,128)(2,1)} custom-call(s32[2]{0:T(128)} %pad_add_fusion.2.refs_0_, bf16[1600,256]{1,0:T(8,128)(2,1)} %get-tuple-element.48.refs_1_, bf16[1600,256]{1,0:T(8,128)(2,1)} %collective-permute-done.11.refs_2_, bf16[2048,1536]{1,0:T(8,128)(2,1)} %shard_map.42.refs_3_.refs_4_.refs_5_.refs_6_, ...), custom_call_target="tpu_custom_call" | custom-call | flops 1610612736 | bytes 7340032 | tf_op jit(solution)/shard_map/pallas_call | solution.py:37
  222.5 6.2 %shard_map.45 = (bf16[2,688,256]{2,1,0:T(8,128)(2,1)}, bf16[2,208,256]{2,1,0:T(8,128)(2,1)}, bf16[2,128,256]{2,1,0:T(8,128)(2,1)}) custom-call(s32[2]{0:T(128)} %pad_add_fusion.3.refs_0_, bf16[1600,256]{1,0:T(8,128)(2,1)} %get-tuple-element.50.refs_1_, bf16[1600,256]{1,0:T(8,128)(2,1)} %copy-done.11, ...), custom_call_target="tpu_custom_call" | custom-call | flops 1610612736 | bytes 7340032 | tf_op jit(solution)/shard_map/pallas_call | solution.py:37
  228.7 2.6 collective-permute-start.14
  231.4 6.1 %shard_map.43 = (bf16[2,688,256]{2,1,0:T(8,128)(2,1)}, bf16[2,208,256]{2,1,0:T(8,128)(2,1)}, bf16[2,128,256]{2,1,0:T(8,128)(2,1)}) custom-call(s32[2]{0:T(128)} %pad_add_fusion.refs_0_, bf16[1600,256]{1,0:T(8,128)(2,1)} %get-tuple-element.43.refs_1_, bf16[1600,256]{1,0:T(8,128)(2,1)} %collective-permute-done.7.refs_2_, ...), custom_call_target="tpu_custom_call" | custom-call | flops 1610612736 | bytes 7340032 | tf_op jit(solution)/shard_map/pallas_call | solution.py:37
  238.4 1.3 collective-permute-start.16
  239.7 6.4 %collective-permute-start.15 = (bf16[2,208,256]{2,1,0:T(8,128)(2,1)}, bf16[2,208,256]{2,1,0:T(8,128)(2,1)S(1)}, u32[]{:S(2)}, u32[]{:S(2)}) collective-permute-start(bf16[2,208,256]{2,1,0:T(8,128)(2,1)} %get-tuple-element.53), channel_id=1, source_target_pairs={{0,6},{2,4},{3,5},{4,2},{6,0},{7,1},{8,14},{10,12},{11,13},{12,10}... | collective-permute-start | bytes 638984 | tf_op jit(solution)/shard_map/ppermute | solution.py:462
  246.1 34.9 %collective-permute-done.16.refs_3_ = bf16[2,128,256]{2,1,0:T(8,128)(2,1)S(1)} collective-permute-done((bf16[2,128,256]{2,1,0:T(8,128)(2,1)}, bf16[2,128,256]{2,1,0:T(8,128)(2,1)S(1)}, u32[]{:S(2)}, u32[]{:S(2)}) %collective-permute-start.16) | collective-permute-done | bytes 131104 | tf_op jit(solution)/shard_map/ppermute | solution.py:462
  281.0 22.1 %collective-permute-start.9 = (bf16[2,208,256]{2,1,0:T(8,128)(2,1)}, bf16[2,208,256]{2,1,0:T(8,128)(2,1)}, u32[]{:S(2)}, u32[]{:S(2)}) collective-permute-start(bf16[2,208,256]{2,1,0:T(8,128)(2,1)} %get-tuple-element.46), channel_id=1, source_target_pairs={{0,4},{1,5},{2,6},{4,0},{5,1},{6,2},{8,12},{9,13},{10,14},{12,8},{... | collective-permute-start | bytes 638984 | tf_op jit(solution)/shard_map/ppermute | solution.py:462
  303.7 3.1 collective-permute-start.10
  306.9 6.2 %shard_map.47.refs_4_ = bf16[4,2048,256]{2,1,0:T(8,128)(2,1)} custom-call(s32[2]{0:T(128)} %pad_add_fusion.4.refs_0_, bf16[1600,256]{1,0:T(8,128)(2,1)} %get-tuple-element.55.refs_1_, bf16[1600,256]{1,0:T(8,128)(2,1)} %collective-permute-done.17.refs_2_, bf16[2048,1536]{1,0:T(8,128)(2,1)} %shard_map.42.refs_3_.refs_4_.refs_5_.refs_6_, ...), custom_call_target="tpu_custom_call" | custom-call | flops 1610612736 | bytes 7340032 | tf_op jit(solution)/shard_map/pallas_call | solution.py:37
  313.1 2.1 shard_map.48.refs_2_
  315.2 2.0 shard_map.49.refs_4_
  318.1 2.0 shard_map.50
  (59 shorter events, 11.5 us)
Async XLA Ops:
  5.3 26.6 %collective-permute-start.5 = (bf16[2048,256]{1,0:T(8,128)(2,1)S(1)}, bf16[2048,256]{1,0:T(8,128)(2,1)}, u32[]{:S(2)}, u32[]{:S(2)}) collective-permute-start(bf16[2048,256]{1,0:T(8,128)(2,1)S(1)} %get-tuple-element.57), channel_id=1, source_target_pairs={{0,2},{1,3},{2,0},{3,1},{4,6},{5,7},{6,4},{7,5},{8,10},{9,11},{10,... | collective-permute-start | bytes 3145736 | tf_op jit(solution)/shard_map/ppermute | solution.py:462
  8.4 128.2 %collective-permute-start.4 = (bf16[2048,256]{1,0:T(8,128)(2,1)}, bf16[2048,256]{1,0:T(8,128)(2,1)}, u32[]{:S(2)}, u32[]{:S(2)}) collective-permute-start(bf16[2048,256]{1,0:T(8,128)(2,1)} %get-tuple-element.58.refs_4_.refs_5_), channel_id=1, source_target_pairs={{0,1},{1,0},{2,3},{3,2},{4,5},{5,4},{6,7},{7,6},{8,9},{9,8},{10,11... | collective-permute-start | bytes 3145736 | tf_op jit(solution)/shard_map/ppermute | solution.py:462
  8.4 49.2 %collective-permute-start.2 = (bf16[2048,256]{1,0:T(8,128)(2,1)S(1)}, bf16[2048,256]{1,0:T(8,128)(2,1)}, u32[]{:S(2)}, u32[]{:S(2)}) collective-permute-start(bf16[2048,256]{1,0:T(8,128)(2,1)S(1)} %get-tuple-element.59), channel_id=1, source_target_pairs={{0,6},{1,7},{2,4},{3,5},{4,2},{5,3},{6,0},{7,1},{8,14},{9,15},{10,... | collective-permute-start | bytes 3145736 | tf_op jit(solution)/shard_map/ppermute | solution.py:462
  10.9 91.5 %collective-permute-start = (bf16[2048,256]{1,0:T(8,128)(2,1)}, bf16[2048,256]{1,0:T(8,128)(2,1)}, u32[]{:S(2)}, u32[]{:S(2)}) collective-permute-start(bf16[2048,256]{1,0:T(8,128)(2,1)} %dynamic-slice_bitcast_fusion.3), channel_id=1, source_target_pairs={{0,4},{1,5},{2,6},{3,7},{4,0},{5,1},{6,2},{7,3},{8,12},{9,13},{10,... | collective-permute-start | bytes 3145736 | tf_op jit(solution)/shard_map/ppermute | solution.py:462
  31.9 107.8 %collective-permute-start.6 = (bf16[2048,256]{1,0:T(8,128)(2,1)}, bf16[2048,256]{1,0:T(8,128)(2,1)}, u32[]{:S(2)}, u32[]{:S(2)}) collective-permute-start(bf16[2048,256]{1,0:T(8,128)(2,1)} %collective-permute-done.5.refs_4_.refs_5_), channel_id=1, source_target_pairs={{0,1},{1,0},{2,3},{3,2},{4,5},{5,4},{6,7},{7,6},{8,9},{9,8},{10,11... | collective-permute-start | bytes 3145736 | tf_op jit(solution)/shard_map/ppermute | solution.py:462
  57.5 85.4 %collective-permute-start.3 = (bf16[2048,256]{1,0:T(8,128)(2,1)}, bf16[2048,256]{1,0:T(8,128)(2,1)}, u32[]{:S(2)}, u32[]{:S(2)}) collective-permute-start(bf16[2048,256]{1,0:T(8,128)(2,1)} %collective-permute-done.2.refs_4_.refs_5_), channel_id=1, source_target_pairs={{0,1},{1,0},{2,3},{3,2},{4,5},{5,4},{6,7},{7,6},{8,9},{9,8},{10,11... | collective-permute-start | bytes 3145736 | tf_op jit(solution)/shard_map/ppermute | solution.py:462
  102.3 54.9 %collective-permute-start.1 = (bf16[2048,256]{1,0:T(8,128)(2,1)}, bf16[2048,256]{1,0:T(8,128)(2,1)}, u32[]{:S(2)}, u32[]{:S(2)}) collective-permute-start(bf16[2048,256]{1,0:T(8,128)(2,1)} %collective-permute-done.refs_4_.refs_5_), channel_id=1, source_target_pairs={{0,1},{1,0},{2,3},{3,2},{4,5},{5,4},{6,7},{7,6},{8,9},{9,8},{10,11... | collective-permute-start | bytes 3145736 | tf_op jit(solution)/shard_map/ppermute | solution.py:462
  102.3 1.9 copy-start
  106.5 0.9 copy-start.3
  125.1 1.9 copy-start.1
  129.3 0.9 copy-start.7
  132.5 0.9 copy-start.4
  135.7 0.9 copy-start.5
  138.9 0.9 copy-start.8
  142.0 0.9 copy-start.10
  145.2 0.9 copy-start.6
  157.2 1.9 copy-start.2
  161.4 0.9 copy-start.9
  195.7 19.1 %collective-permute-start.11 = (bf16[1600,256]{1,0:T(8,128)(2,1)}, bf16[1600,256]{1,0:T(8,128)(2,1)}, u32[]{:S(2)}, u32[]{:S(2)}) collective-permute-start(bf16[1600,256]{1,0:T(8,128)(2,1)} %get-tuple-element.49), channel_id=1, source_target_pairs={{0,1},{1,0},{2,3},{3,2},{4,5},{5,4},{6,7},{7,6},{8,9},{9,8},{10,11... | collective-permute-start | bytes 2457608 | tf_op jit(solution)/shard_map/ppermute | solution.py:462
  196.8 24.8 %collective-permute-start.13 = (bf16[1600,256]{1,0:T(8,128)(2,1)}, bf16[1600,256]{1,0:T(8,128)(2,1)S(1)}, u32[]{:S(2)}, u32[]{:S(2)}) collective-permute-start(bf16[1600,256]{1,0:T(8,128)(2,1)} %get-tuple-element.51), channel_id=1, source_target_pairs={{0,1},{1,0},{2,3},{3,2},{4,5},{5,4},{6,7},{7,6},{8,9},{9,8},{10,11... | collective-permute-start | bytes 2457608 | tf_op jit(solution)/shard_map/ppermute | solution.py:462
  197.5 33.8 %collective-permute-start.7 = (bf16[1600,256]{1,0:T(8,128)(2,1)}, bf16[1600,256]{1,0:T(8,128)(2,1)}, u32[]{:S(2)}, u32[]{:S(2)}) collective-permute-start(bf16[1600,256]{1,0:T(8,128)(2,1)} %get-tuple-element.44), channel_id=1, source_target_pairs={{0,1},{1,0},{2,3},{3,2},{4,5},{5,4},{6,7},{7,6},{8,9},{9,8},{10,11... | collective-permute-start | bytes 2457608 | tf_op jit(solution)/shard_map/ppermute | solution.py:462
  214.8 24.9 %collective-permute-start.17 = (bf16[1600,256]{1,0:T(8,128)(2,1)}, bf16[1600,256]{1,0:T(8,128)(2,1)}, u32[]{:S(2)}, u32[]{:S(2)}) collective-permute-start(bf16[1600,256]{1,0:T(8,128)(2,1)} %get-tuple-element.56), channel_id=1, source_target_pairs={{0,1},{1,0},{2,3},{3,2},{4,5},{5,4},{6,7},{7,6},{8,9},{9,8},{10,11... | collective-permute-start | bytes 2457608 | tf_op jit(solution)/shard_map/ppermute | solution.py:462
  221.0 94.1 %collective-permute-start.12 = (bf16[2,1024,256]{2,1,0:T(8,128)(2,1)}, bf16[2,1024,256]{2,1,0:T(8,128)(2,1)}, u32[]{:S(2)}, u32[]{:S(2)}) collective-permute-start(bf16[2,1024,256]{2,1,0:T(8,128)(2,1)} %shard_map.44), channel_id=1, source_target_pairs={{0,2},{1,3},{2,0},{3,1},{4,6},{5,7},{6,4},{7,5},{8,10},{9,11},{10,... | collective-permute-start | bytes 3145736 | tf_op jit(solution)/shard_map/ppermute | solution.py:462
  221.6 0.9 copy-start.11
  228.7 84.4 %collective-permute-start.14 = (bf16[2,688,256]{2,1,0:T(8,128)(2,1)}, bf16[2,688,256]{2,1,0:T(8,128)(2,1)}, u32[]{:S(2)}, u32[]{:S(2)}) collective-permute-start(bf16[2,688,256]{2,1,0:T(8,128)(2,1)} %get-tuple-element.52), channel_id=1, source_target_pairs={{0,6},{1,7},{2,4},{3,5},{4,2},{5,3},{6,0},{7,1},{8,14},{9,15},{10,... | collective-permute-start | bytes 2113544 | tf_op jit(solution)/shard_map/ppermute | solution.py:462
  237.5 79.7 %collective-permute-start.8 = (bf16[2,688,256]{2,1,0:T(8,128)(2,1)}, bf16[2,688,256]{2,1,0:T(8,128)(2,1)S(1)}, u32[]{:S(2)}, u32[]{:S(2)}) collective-permute-start(bf16[2,688,256]{2,1,0:T(8,128)(2,1)} %get-tuple-element.45), channel_id=1, source_target_pairs={{0,4},{1,5},{2,6},{3,7},{4,0},{5,1},{6,2},{7,3},{8,12},{9,13},{10,... | collective-permute-start | bytes 2113544 | tf_op jit(solution)/shard_map/ppermute | solution.py:462
  238.4 42.6 %collective-permute-start.16 = (bf16[2,128,256]{2,1,0:T(8,128)(2,1)}, bf16[2,128,256]{2,1,0:T(8,128)(2,1)S(1)}, u32[]{:S(2)}, u32[]{:S(2)}) collective-permute-start(bf16[2,128,256]{2,1,0:T(8,128)(2,1)} %get-tuple-element.54), channel_id=1, source_target_pairs={{2,4},{3,5},{6,0},{7,1},{10,12},{11,13},{14,8},{15,9},{18,20},{19,... | collective-permute-start | bytes 393224 | tf_op jit(solution)/shard_map/ppermute | solution.py:462
  239.7 64.0 %collective-permute-start.15 = (bf16[2,208,256]{2,1,0:T(8,128)(2,1)}, bf16[2,208,256]{2,1,0:T(8,128)(2,1)S(1)}, u32[]{:S(2)}, u32[]{:S(2)}) collective-permute-start(bf16[2,208,256]{2,1,0:T(8,128)(2,1)} %get-tuple-element.53), channel_id=1, source_target_pairs={{0,6},{2,4},{3,5},{4,2},{6,0},{7,1},{8,14},{10,12},{11,13},{12,10}... | collective-permute-start | bytes 638984 | tf_op jit(solution)/shard_map/ppermute | solution.py:462
  281.0 22.7 %copy-start.14 = (bf16[2,128,256]{2,1,0:T(8,128)(2,1)}, bf16[2,128,256]{2,1,0:T(8,128)(2,1)S(1)}, u32[]{:S(2)}) copy-start(bf16[2,128,256]{2,1,0:T(8,128)(2,1)S(1)} %collective-permute-done.16.refs_3_) | copy-start | bytes 393220
  281.0 36.2 %collective-permute-start.9 = (bf16[2,208,256]{2,1,0:T(8,128)(2,1)}, bf16[2,208,256]{2,1,0:T(8,128)(2,1)}, u32[]{:S(2)}, u32[]{:S(2)}) collective-permute-start(bf16[2,208,256]{2,1,0:T(8,128)(2,1)} %get-tuple-element.46), channel_id=1, source_target_pairs={{0,4},{1,5},{2,6},{4,0},{5,1},{6,2},{8,12},{9,13},{10,14},{12,8},{... | collective-permute-start | bytes 638984 | tf_op jit(solution)/shard_map/ppermute | solution.py:462
  303.7 9.3 %copy-start.13 = (bf16[2,208,256]{2,1,0:T(8,128)(2,1)}, bf16[2,208,256]{2,1,0:T(8,128)(2,1)S(1)}, u32[]{:S(2)}) copy-start(bf16[2,208,256]{2,1,0:T(8,128)(2,1)S(1)} %collective-permute-done.15.refs_2_) | copy-start | bytes 638980
  303.7 13.5 %collective-permute-start.10 = (bf16[2,128,256]{2,1,0:T(8,128)(2,1)}, bf16[2,128,256]{2,1,0:T(8,128)(2,1)}, u32[]{:S(2)}, u32[]{:S(2)}) collective-permute-start(bf16[2,128,256]{2,1,0:T(8,128)(2,1)} %get-tuple-element.47), channel_id=1, source_target_pairs={{0,4},{1,5},{4,0},{5,1},{8,12},{9,13},{12,8},{13,9},{16,20},{17,21... | collective-permute-start | bytes 393224 | tf_op jit(solution)/shard_map/ppermute | solution.py:462
  317.2 0.9 copy-start.12
